TPU v7x, 8 devices: a whole 2x2x1 slice. The times are simulated.
8 devices in a mesh: data: 2 (over z, y), expert: 4 (over x, core).
Axes of the slice: x: 2, y: 2, z: 1, core: 2. Of those that a mesh axis runs over, the one named last changes fastest.
Arguments:
- x: bfloat16 [16384, 4096], P(('data', 'expert')), parts along dimension 0
- idx: int32 [16384, 2], P(('data', 'expert')), parts along dimension 0
- wr: bfloat16 [4096, 8], replicated
- w1: bfloat16 [8, 4096, 6400], P('expert')
- w3: bfloat16 [8, 4096, 6400], P('expert')
- w2: bfloat16 [8, 6400, 4096], P('expert')
Outputs:
- output: bfloat16 [16384, 4096], P(('data', 'expert')), parts along dimension 0
There are 2 independent parts. A program takes and returns all parts, laid end to end along the dimension named above; an argument that names none is the same for every part.
All inputs are finite; a program needn't handle non-finite values.
Results may differ from a plain program's by a relative error of at most 0.001.
Values are sent between devices in bfloat16 or wider.
A program may use at most 1.5 GiB of HBM per device.

v0:
```python
import jax
import jax.numpy as jnp
from jax import lax
from jax.sharding import PartitionSpec as P


def _mlp(buf, w1, w3, w2):
    a = jnp.einsum('ecd,edf->ecf', buf, w1, preferred_element_type=jnp.float32)
    b = jnp.einsum('ecd,edf->ecf', buf, w3, preferred_element_type=jnp.float32)
    h = (jax.nn.silu(a) * b).astype(jnp.bfloat16)
    return jnp.einsum('ecf,efd->ecd', h, w2, preferred_element_type=jnp.float32).astype(jnp.bfloat16)


def solution(mesh):
    n = mesh.shape['expert']

    def local(x, idx, wr, w1, w3, w2):
        t, d = x.shape
        k = idx.shape[1]
        e_all = wr.shape[1]
        epd = w1.shape[0]
        cs = 2 * k * t // e_all
        p = t * k
        rows = e_all * cs
        logits = jnp.dot(x, wr, preferred_element_type=jnp.float32)
        ids = jnp.arange(e_all, dtype=jnp.int32)
        g = jax.nn.softmax(jnp.sum(jnp.where(idx[:, :, None] == ids, logits[:, None, :], 0.0), axis=2), axis=-1)
        e = idx.reshape(-1)
        oh = e[:, None] == ids[None, :]
        q = jnp.arange(p, dtype=jnp.int32)
        tri = (q[None, :] <= q[:, None]).astype(jnp.bfloat16)
        cnt = jnp.dot(tri, oh.astype(jnp.bfloat16), preferred_element_type=jnp.float32)
        pos = jnp.sum(jnp.where(oh, cnt, 0.0), axis=1).astype(jnp.int32) - 1
        valid = pos < cs
        dest = jnp.where(valid, e * cs + pos, rows)
        r = jnp.arange(rows, dtype=jnp.int32)
        dm = jnp.any(r[:, None, None] == dest.reshape(t, k)[None], axis=2).astype(x.dtype)
        send = jnp.dot(dm, x, preferred_element_type=x.dtype)
        recv = lax.all_to_all(send, 'expert', 0, 0, tiled=True)
        buf = recv.reshape(n, epd, cs, d).transpose(1, 0, 2, 3).reshape(epd, n * cs, d)
        out = _mlp(buf, w1, w3, w2)
        out = out.reshape(epd, n, cs, d).transpose(1, 0, 2, 3).reshape(n * epd * cs, d)
        back = lax.all_to_all(out, 'expert', 0, 0, tiled=True)
        sel = (dest[:, None] == r[None, :]).astype(x.dtype)
        op = jnp.dot(sel, back, preferred_element_type=back.dtype)
        y = jnp.sum(g[:, :, None] * op.reshape(t, k, d).astype(jnp.float32), axis=1)
        return y.astype(x.dtype)

    tok = P(('data', 'expert'), None)
    wsp = P('expert', None, None)
    return jax.shard_map(local, mesh=mesh, in_specs=(tok, tok, P(), wsp, wsp, wsp), out_specs=tok, check_vma=False)
```

profile of v0, /device:TPU:0, one launch (start us, length us, event | category | flops | bytes accessed | tf_op | source)
XLA Modules:
  0.0 3471.1 jit_solution(6297981113560753337)
XLA Ops:
  0.0 0.0 copy-start
  0.0 0.8 broadcast_multiply_fusion
  0.8 1.1 copy.19
  1.8 0.4 copy.21
  2.2 0.5 eq.73
  2.7 15.0 fusion.13
  17.7 1.0 sub.21
  18.7 0.1 add_select_fusion
  18.9 0.3 copy.22
  19.2 0.0 copy-start.2
  19.2 37.9 %fusion.3 = pred[8192,2048]{1,0:T(32,128)(4,1)} fusion(s32[2048,2]{0,1:T(2,128)S(1)} %copy.22), kind=kLoop, calls=%fused_computation.5 | loop fusion | flops 50331648 | bytes 16793600 | tf_op jit(solution)/shard_map/reduce_or | solution.py:37
  57.1 148.3 %fusion.10 = bf16[4,2048,4096]{2,1,0:T(8,128)(2,1)} fusion(pred[4,2048,2048]{2,1,0:T(32,128)(4,1)} %bitcast.33, bf16[2048,4096]{1,0:T(8,128)(2,1)} %param.6), kind=kOutput, calls=%fused_computation.12 | convolution fusion | flops 137438953472 | bytes 100663296 | tf_op jit(solution)/shard_map/dot_general | solution.py:38
  205.5 0.0 copy-done.2
  205.5 755.9 %all_to_all.18 = bf16[4,2048,4096]{2,1,0:T(8,128)(2,1)} all-to-all(bf16[4,2048,4096]{2,1,0:T(8,128)(2,1)} %fusion.10), channel_id=1, replica_groups=mesh['data'=2,'expert'=4] {'expert'}, dimensions={0} | all-to-all | bytes 134217728 | tf_op jit(solution)/shard_map/all_to_all | solution.py:39
  961.4 44.0 %copy.24 = bf16[2,4,1024,4096]{3,2,1,0:T(8,128)(2,1)} copy(bf16[2,4,1024,4096]{3,2,0,1:T(8,128)(2,1)} %bitcast.4) | data formatting | bytes 134217728 | tf_op jit(solution)/shard_map/transpose | solution.py:40
  1005.3 448.0 %fusion.20 = f32[2,4096,6400]{2,1,0:T(8,128)} fusion(bf16[2,4096,4096]{2,1,0:T(8,128)(2,1)} %bitcast.5, bf16[2,4096,6400]{2,1,0:T(8,128)(2,1)} %param.10), kind=kOutput, calls=%fused_computation.29 | convolution fusion | flops 429496729600 | bytes 381681664 | tf_op jit(solution)/shard_map/ecd,edf->ecf/dot_general | solution.py:9
  1453.3 448.2 %fusion.19 = f32[2,4096,6400]{2,1,0:T(8,128)} fusion(bf16[2,4096,4096]{2,1,0:T(8,128)(2,1)} %bitcast.5, bf16[2,4096,6400]{2,1,0:T(8,128)(2,1)} %param.9), kind=kOutput, calls=%fused_computation.28 | convolution fusion | flops 429496729600 | bytes 381681664 | tf_op jit(solution)/shard_map/ecd,edf->ecf/dot_general | solution.py:8
  1901.5 476.5 %fusion.7 = bf16[2,4096,4096]{2,1,0:T(8,128)(2,1)} fusion(bf16[2,6400,4096]{2,1,0:T(8,128)(2,1)} %param.11, f32[2,4096,6400]{2,1,0:T(8,128)} %fusion.20, f32[2,4096,6400]{2,1,0:T(8,128)} %fusion.19), kind=kOutput, calls=%fused_computation.11 | convolution fusion | flops 429844856832 | bytes 591396864 | tf_op jit(solution)/shard_map/ecf,efd->ecd/dot_general | solution.py:11
  2378.0 44.4 %copy.25 = bf16[2,4,1024,4096]{3,2,0,1:T(8,128)(2,1)} copy(bf16[2,4,1024,4096]{3,2,1,0:T(8,128)(2,1)} %bitcast.6) | data formatting | bytes 134217728 | tf_op jit(solution)/shard_map/reshape | solution.py:42
  2422.4 0.0 copy-start.1
  2422.4 0.0 copy-start.3
  2422.4 13.4 all-to-all-start.1
  2435.8 0.0 copy-done
  2435.8 10.2 fusion.18
  2446.0 0.0 copy-done.1
  2446.0 0.1 select_reduce_fusion
  2446.2 711.6 %all-to-all-done.1 = bf16[4,2048,4096]{2,1,0:T(8,128)(2,1)} async-done(((bf16[4,2048,4096]{2,1,0:T(8,128)(2,1)}), bf16[4,2048,4096]{2,1,0:T(8,128)(2,1)}, u32[]{:S(2)}, u32[]{:S(2)}) %all-to-all-start.1) | async-done | bytes 67108896 | tf_op jit(solution)/shard_map/all_to_all | solution.py:43
  3157.8 0.0 copy-done.3
  3157.8 313.1 %multiply_reduce_fusion = bf16[2048,4096]{1,0:T(8,128)(2,1)} fusion(f32[2048,2]{0,1:T(2,128)S(1)} %fusion.15, bf16[8192,4096,1]{1,0,2:T(8,128)(2,1)} %bitcast.10, s32[2048,2]{0,1:T(2,128)S(1)} %copy-done.3), kind=kOutput, calls=%fused_computation.7 | convolution fusion | flops 274953404416 | bytes 83918848 | tf_op jit(solution)/shard_map/dot_general | solution.py:45
  (4 shorter events, 0.1 us)
Async XLA Ops:
  0.0 2435.8 %copy-start = (bf16[4096,8]{0,1:T(8,128)(2,1)S(1)}, bf16[4096,8]{0,1:T(8,128)(2,1)}, u32[]{:S(2)}) copy-start(bf16[4096,8]{0,1:T(8,128)(2,1)} %param.8) | copy-start | bytes 196612
  19.2 186.3 %copy-start.2 = (s32[2048,2]{0,1:T(2,128)}, s32[2048,2]{0,1:T(2,128)S(1)}, u32[]{:S(2)}) copy-start(s32[2048,2]{0,1:T(2,128)S(1)} %copy.22) | copy-start | bytes 49156
  2422.4 23.6 copy-start.1
  2422.4 735.4 %copy-start.3 = (s32[2048,2]{0,1:T(2,128)S(1)}, s32[2048,2]{0,1:T(2,128)}, u32[]{:S(2)}) copy-start(s32[2048,2]{0,1:T(2,128)} %copy-done.2) | copy-start | bytes 49156
  2422.4 735.4 %all-to-all-start.1 = ((bf16[4,2048,4096]{2,1,0:T(8,128)(2,1)}), bf16[4,2048,4096]{2,1,0:T(8,128)(2,1)}, u32[]{:S(2)}, u32[]{:S(2)}) async-start(bf16[4,2048,4096]{2,1,0:T(8,128)(2,1)} %bitcast.8), calls=%async_computation.1 | async-start | bytes 134217728 | tf_op jit(solution)/shard_map/all_to_all | solution.py:43
where the time goes:
time: 3480 us; the launch traced here: 3470 us
  matrix products  1860 us (53%)
  blocking collectives  756 us (22%)
  waiting for transfers between devices  712 us (20%)
  local copies, waits for them, and re-layouts  91.7 us (3%)
  other arithmetic  39 us (1%)
    all_to_all x1, blocking collectives, local(): recv = lax.all_to_all(send, 'expert', 0, 0, tiled=True)  756 us
    all_to_all x1, waiting for transfers between devices, local(): back = lax.all_to_all(out, 'expert', 0, 0, tiled=True)  712 us
    dot_general x1, matrix products, _mlp(): jnp.einsum('ecf,efd->ecd', h, w2, preferred_element_type=jnp.float32)  476 us
    dot_general x1, matrix products, _mlp(): a = jnp.einsum('ecd,edf->ecf', buf, w1, preferred_element_type=jnp.float32)  448 us
    dot_general x1, matrix products, _mlp(): b = jnp.einsum('ecd,edf->ecf', buf, w3, preferred_element_type=jnp.float32)  448 us
    dot_general x1, matrix products, local(): op = jnp.dot(sel, back, preferred_element_type=back.dtype)  313 us
    dot_general x1, matrix products, local(): send = jnp.dot(dm, x, preferred_element_type=x.dtype)  148 us
  transfers between devices with their start and end apart: 1, of which 1 were waited for; matrix products, arithmetic and copies ran while one was open for 0% of the time, Pallas kernels for 0%

commit v1 on v0

v1 whole, which is shorter than its diff:
```python
import functools

import jax
import jax.numpy as jnp
from jax import lax
from jax.experimental import pallas as pl
from jax.experimental.pallas import tpu as pltpu
from jax.sharding import PartitionSpec as P

VMEM_BYTES = 67043328
LANES = 128
SB = 1024
GRAN = 128
UNIT = 512
TAILS = (128, 256, 384)
CHUNK = 256
CAP = 416
MORE = 152
BN1 = 256
BN2 = 256


def _for_rows(count, fn):
    unit = UNIT // GRAN
    whole = lax.div(count, unit)

    def body(i, c):
        fn(pl.multiple_of(i * UNIT, UNIT), UNIT)
        return c

    lax.fori_loop(0, whole, body, 0)
    rest = count - whole * unit
    for tail in TAILS:
        @pl.when(rest == tail // GRAN)
        def _():
            fn(pl.multiple_of(whole * UNIT, UNIT), tail)


def _ffn_kernel(n1, blk, sub, ex, x_ref, w1_ref, w3_ref, w2_ref, o_ref, h_ref):
    s, j = pl.program_id(0), pl.program_id(1)
    count = sub[s]

    @pl.when(j < n1)
    def _():
        col = pl.multiple_of(j * BN1, BN1)

        def up(r, m):
            x = x_ref[pl.ds(r, m), :]
            a = jnp.dot(x, w1_ref[0], preferred_element_type=jnp.float32)
            b = jnp.dot(x, w3_ref[0], preferred_element_type=jnp.float32)
            h_ref[pl.ds(r, m), pl.ds(col, BN1)] = (a * jax.nn.sigmoid(a) * b).astype(h_ref.dtype)
        _for_rows(count, up)

    @pl.when(j >= n1)
    def _():
        def down(r, m):
            o = jnp.dot(h_ref[pl.ds(r, m), :], w2_ref[0], preferred_element_type=jnp.float32)
            o_ref[pl.ds(r, m), :] = o.astype(o_ref.dtype)
        _for_rows(count, down)


def _ffn(xs, w1, w3, w2, meta, rows_out, rows_hint):
    blk, sub, ex = meta
    d, f = w1.shape[1], w1.shape[2]
    n1, n2 = f // BN1, d // BN2
    at = lambda s, j, sub: jnp.where(sub[s] > 0, j, n1 + n2 - 1)
    up = lambda s, j, sub: jnp.minimum(at(s, j, sub), n1 - 1)
    down = lambda s, j, sub: jnp.maximum(at(s, j, sub) - n1, 0)
    return pl.pallas_call(
        functools.partial(_ffn_kernel, n1),
        out_shape=jax.ShapeDtypeStruct((rows_out, d), xs.dtype),
        grid_spec=pltpu.PrefetchScalarGridSpec(
            num_scalar_prefetch=3,
            grid=(blk.shape[0], n1 + n2),
            in_specs=[
                pl.BlockSpec((SB, d), lambda s, j, blk, sub, ex: (blk[s], 0)),
                pl.BlockSpec((1, d, BN1), lambda s, j, blk, sub, ex: (ex[s], 0, up(s, j, sub))),
                pl.BlockSpec((1, d, BN1), lambda s, j, blk, sub, ex: (ex[s], 0, up(s, j, sub))),
                pl.BlockSpec((1, f, BN2), lambda s, j, blk, sub, ex: (ex[s], 0, down(s, j, sub))),
            ],
            out_specs=pl.BlockSpec((SB, BN2), lambda s, j, blk, sub, ex: (blk[s], down(s, j, sub))),
            scratch_shapes=[pltpu.VMEM((SB, f), xs.dtype)],
        ),
        compiler_params=pltpu.CompilerParams(
            vmem_limit_bytes=VMEM_BYTES, dimension_semantics=("arbitrary", "arbitrary")),
        cost_estimate=pl.CostEstimate(
            flops=6 * rows_hint * d * f, bytes_accessed=12 * d * f, transcendentals=rows_hint * f),
        name="ffn",
    )(blk, sub, ex, xs, w1, w3, w2)


def _unwritten(shape, dtype):
    return pl.pallas_call(
        lambda o: None, out_shape=jax.ShapeDtypeStruct(shape, dtype),
        out_specs=pl.BlockSpec(memory_space=pl.ANY), name="unwritten")()


def _pad8(n):
    return (n + 7) & ~7


def _row_list(incl, off, end, rows):
    c = incl.shape[0]
    r = jnp.arange(rows, dtype=jnp.int32)
    chunk = jnp.sum((end[None, :] <= r[:, None]).astype(jnp.int32), axis=1)
    hot = chunk[:, None] == jnp.arange(c, dtype=jnp.int32)[None, :]
    start = jnp.sum(jnp.where(hot, off[None, :], 0), axis=1)
    cum = jnp.dot(hot.astype(jnp.bfloat16), incl.astype(jnp.bfloat16), preferred_element_type=jnp.float32)
    lane = jnp.sum((cum <= (r - start).astype(jnp.float32)[:, None]).astype(jnp.int32), axis=1)
    return jnp.minimum(chunk * LANES + lane, c * LANES - 1)


def _meta(counts, per):
    epd = counts.shape[0]
    i = jnp.arange(epd * per, dtype=jnp.int32)
    n = jnp.broadcast_to(counts[:, None], (epd, per)).reshape(-1)
    sub = jnp.clip(lax.div(n - lax.rem(i, per) * SB + GRAN - 1, GRAN), 0, SB // GRAN)
    live = sub > 0
    slot = jnp.sum((live[None, :] & (i[None, :] < i[:, None])).astype(jnp.int32), axis=1)
    live_n = jnp.sum(live.astype(jnp.int32))
    put = (slot[None, :] == jnp.minimum(i, live_n - 1)[:, None]) & live[None, :]
    pick = lambda v: jnp.sum(jnp.where(put, v[None, :], 0), axis=1).astype(jnp.int32)
    return pick(i), jnp.where(i < live_n, pick(sub), 0), pick(lax.div(i, per))


def _gather(src, lists, counts, buf):
    epd, cap = lists.shape
    flat = lists.reshape(-1)
    nch = lax.div(counts + CHUNK - 1, CHUNK)
    ends = [jnp.sum(nch[:e + 1]) for e in range(epd)]

    def body(i, buf):
        row = i * CHUNK
        for e in range(1, epd):
            row = jnp.where(i >= ends[e - 1], e * cap + (i - ends[e - 1]) * CHUNK, row)
        rows = lax.dynamic_slice(flat, (row,), (CHUNK,))
        part = src.at[rows].get(mode='promise_in_bounds')
        return lax.dynamic_update_slice(buf, part, (row, 0))

    return lax.fori_loop(0, ends[-1], body, buf)


def solution(mesh):
    n = mesh.shape['expert']

    def local(x, idx, wr, w1, w3, w2):
        t, d = x.shape
        k = idx.shape[1]
        e_all = wr.shape[1]
        epd = w1.shape[0]
        cs = 2 * k * t // e_all
        half = t // 2
        nc = t // LANES
        hc = nc // 2
        me = lax.axis_index('expert')
        sib = me ^ 1
        far = (me ^ 2) & ~1
        i32 = jnp.int32

        idx_t = idx.T
        idx_g = lax.all_gather(idx_t, ('data', 'expert'))
        xg, idx_g = lax.optimization_barrier((x, idx_g))
        idx_all = lax.dynamic_slice_in_dim(idx_g, lax.axis_index('data') * n, n, axis=0)
        x_h = [lax.all_gather(xg[h * half:(h + 1) * half], 'expert', tiled=True) for h in range(2)]
        x_sib = lax.ppermute(x, 'expert', [(i, i + 1 - 2 * (i % 2)) for i in range(n)])

        ids = jnp.arange(e_all, dtype=i32)
        hit = jnp.any(idx_all[:, None, :, :] == ids[None, :, None, None], axis=2)
        hit = hit.reshape(n, e_all, nc, LANES)
        lane = jnp.arange(LANES, dtype=i32)
        tri = (lane[:, None] <= lane[None, :]).astype(jnp.bfloat16)
        incl = jnp.dot(hit.astype(jnp.bfloat16), tri, preferred_element_type=jnp.float32).astype(i32)
        tot = incl[..., LANES - 1]
        ch = jnp.arange(nc, dtype=i32)
        off = jnp.sum(jnp.where(ch[None, :] < ch[:, None], tot[:, :, None, :], 0), axis=3)
        n_h = jnp.stack([jnp.sum(tot[..., :hc], axis=-1), jnp.sum(tot[..., hc:], axis=-1)], axis=1)

        dev = jnp.arange(n, dtype=i32)
        e_dev = lax.div(ids, epd)
        own = e_dev == me
        far_e = (e_dev >> 1) != (me >> 1)
        extra = cs - CAP
        far_base = 2 * epd * cs
        over_base = far_base + 2 * 2 * epd * CAP
        buf_rows = -(-(over_base + 2 * 2 * epd * extra) // SB) * SB

        take1 = lambda a, i: lax.dynamic_index_in_dim(a, i, 0, keepdims=False)
        mine = lambda a: lax.dynamic_slice_in_dim(a, me * epd, epd, axis=1)

        my_off, my_incl = take1(off, me), take1(incl, me)
        my_hit = take1(hit, me).astype(i32)
        rank = (my_incl - my_hit + my_off[:, :, None]).reshape(e_all, t)
        my_n0 = take1(n_h, me)[0]
        second = (jnp.arange(t, dtype=i32) >= half)[None, :]
        cross = ((e_dev ^ me) & 1) == 1
        slot = cross.astype(i32) * epd + lax.rem(ids, epd)
        far_rank = rank - jnp.where(second, my_n0[:, None], 0)
        far_slot = second.astype(i32) * 2 * epd + slot[:, None]
        far_place = jnp.where(far_rank < CAP, far_base + far_slot * CAP + far_rank,
                              over_base + far_slot * extra + far_rank - CAP)
        near_place = jnp.where(own, lax.rem(ids, epd), epd + lax.rem(ids, epd))[:, None] * cs + rank
        place = jnp.where(far_e[:, None], far_place, near_place)
        pos = jnp.sum(jnp.where(idx_t[:, None, :] == ids[None, :, None], place[None], 0), axis=1)

        incl_l, off_l, tot_l = mine(incl), mine(off), mine(tot)
        n_hl = lax.dynamic_slice_in_dim(n_h, me * epd, epd, axis=2)

        def one_source(s):
            a, o, tt = take1(incl_l, s), take1(off_l, s), take1(tot_l, s)
            return jnp.stack([_row_list(a[e], o[e], o[e] + tt[e], cs) for e in range(epd)]), take1(n_hl, s).sum(axis=0)

        def far_half(h):
            sl = slice(h * hc, (h + 1) * hc)
            pick = lambda a: jnp.moveaxis(lax.dynamic_slice_in_dim(a, far, 2, axis=0)[:, :, sl], 0, 1)
            a, tt = pick(incl_l), pick(tot_l)
            cnt = lax.dynamic_slice_in_dim(n_hl, far, 2, axis=0)[:, h]
            o = pick(off_l) - (lax.dynamic_slice_in_dim(n_hl, far, 2, axis=0)[:, 0].T[:, :, None] if h else 0)
            p0 = _pad8(cnt[0])
            o = o + jnp.stack([jnp.zeros_like(p0), p0], axis=1)[:, :, None]
            o = o.reshape(epd, nc)
            end = jnp.concatenate([o[:, 1:], (p0 + cnt[1])[:, None]], axis=1)
            a = a.reshape(epd, nc, LANES)
            lst = jnp.stack([_row_list(a[e], o[e], end[e], 2 * cs) for e in range(epd)])
            return lst + far * half, p0 + cnt[1]

        l_own, c_own = one_source(me)
        l_sib, c_sib = one_source(sib)
        l_far, c_far = zip(far_half(0), far_half(1))

        logits = jnp.dot(x, wr, preferred_element_type=jnp.float32)
        g = jax.nn.softmax(jnp.sum(jnp.where(idx[:, :, None] == ids, logits[:, None, :], 0.0), axis=2), axis=-1)

        hint = t * k * n // e_all * epd // 4
        perm = {m: [(i, i ^ m) for i in range(n)] for m in (1, 2, 3)}

        hit_g = jnp.any(idx_g[:, None, :, :] == ids[:, None, None], axis=2)
        most = jnp.max(jnp.sum(hit_g.reshape(-1, 2, half).astype(i32), axis=2))
        steps = jnp.maximum(lax.div(most - CAP + MORE - 1, MORE), 0)

        def start_of(h, home, e):
            first = jnp.where((home & 1) == 1, _pad8(take1(n_hl, home & ~1)[h, e]), 0)
            return pl.multiple_of(e * 2 * cs + first, 8)

        def pack(o, h, m, lo, size):
            home = me ^ m
            return jnp.concatenate([lax.dynamic_slice(o, (start_of(h, home, e) + lo, 0), (size, d)) for e in range(epd)])

        def far_rows(o, h, m, lo, size):
            return lax.ppermute(pack(o, h, m, lo, size), 'expert', perm[m])

        xs = x_sib.at[l_sib.reshape(-1)].get(mode='promise_in_bounds')
        o_sib = _ffn(xs, w1, w3, w2, _meta(c_sib, cs // SB), epd * cs, hint)
        r_sib = lax.ppermute(o_sib, 'expert', perm[1])
        out, o_far, r_far = [o_sib], [], []
        for h in range(2):
            lst, out = lax.optimization_barrier((l_far[h], out))
            xs = _gather(x_h[h], lst, c_far[h], _unwritten((epd * 2 * cs, d), x.dtype))
            last = _ffn(xs, w1, w3, w2, _meta(c_far[h], 2 * cs // SB), epd * 2 * cs + SB, hint)
            o_far.append(last)
            out = [pack(last, h, m, 0, CAP) for m in (2, 3)]
            r_far.append([lax.ppermute(o, 'expert', perm[m]) for o, m in zip(out, (2, 3))])
        lst, out, r_far[0] = lax.optimization_barrier((l_own, out, r_far[0]))
        xs = x.at[lst.reshape(-1)].get(mode='promise_in_bounds')
        buf = _ffn(xs, w1, w3, w2, _meta(c_own, cs // SB), buf_rows, hint)

        buf = lax.dynamic_update_slice(buf, r_sib, (epd * cs, 0))
        for h in range(2):
            for i in range(2):
                buf = lax.dynamic_update_slice(buf, r_far[h][i], (far_base + (2 * h + i) * epd * CAP, 0))

        def more(step, buf):
            for h in range(2):
                for i, m in enumerate((2, 3)):
                    lo = jnp.minimum(CAP + step * MORE, cs - MORE)
                    got = far_rows(o_far[h], h, m, lo, MORE)
                    for e in range(epd):
                        row = over_base + ((2 * h + i) * epd + e) * extra + lo - CAP
                        buf = lax.dynamic_update_slice(buf, got[e * MORE:(e + 1) * MORE], (row, 0))
            return buf

        buf = lax.fori_loop(0, steps, more, buf)

        op = buf.at[pos.reshape(-1)].get(mode='promise_in_bounds').reshape(k, t, d)
        y = jnp.sum(g.T[:, :, None] * op.astype(jnp.float32), axis=0)
        return y.astype(x.dtype)

    tok = P(('data', 'expert'), None)
    wsp = P('expert', None, None)
    return jax.shard_map(local, mesh=mesh, in_specs=(tok, tok, P(), wsp, wsp, wsp), out_specs=tok, check_vma=False)
```

time: 3480 us -> 1670 us (0.48)
  the two profiles are of different devices: /device:TPU:0 before, /device:TPU:2 now
where the time goes in v1:
time: 1670 us; the launch traced here: 1660 us
  Pallas kernels  952 us (57%)
  local copies, waits for them, and re-layouts  374 us (22%)
  starting transfers between devices  191 us (11%)
  other arithmetic  69.3 us (4%)
  between operations  22.6 us (1%)
  loops' own time  22.5 us (1%)
    pallas_call x4, Pallas kernels, _ffn(): pl.pallas_call(functools.partial(_ffn_kernel, n1), out_shape=jax.ShapeDty...  952 us
    ppermute x4, starting transfers between devices, local(): lax.ppermute(o, 'expert', perm[m])  191 us
    gather x1, local copies, waits for them, and re-layouts, local(): op = buf.at[pos.reshape(-1)].get(mode='promise_in_bounds').reshape(k, t, d)  132 us
    gather x9, local copies, waits for them, and re-layouts, body(): part = src.at[rows].get(mode='promise_in_bounds')  81.4 us
    gather x1, local copies, waits for them, and re-layouts, local(): xs = x_sib.at[l_sib.reshape(-1)].get(mode='promise_in_bounds')  36.8 us
    gather x1, local copies, waits for them, and re-layouts, local(): xs = x.at[lst.reshape(-1)].get(mode='promise_in_bounds')  36.7 us
  transfers between devices with their start and end apart: 8, of which 0 were waited for; matrix products, arithmetic and copies ran while one was open for 17% of the time, Pallas kernels for 57%

profile of v1, /device:TPU:2, one launch (start us, length us, event | category | flops | bytes accessed | tf_op | source)
XLA Modules:
  0.0 1656.1 jit_solution(5598069185727318675)
XLA Ops:
  6.5 11.3 all-gather.1
  17.8 11.7 fusion.108
  31.7 1.2 fusion.100
  50.7 10.2 fusion.112
  71.2 1.2 compare_select_fusion.27.sub
  75.0 36.8 %gather_fusion.2 = bf16[2048,4096]{1,0:T(8,128)(2,1)} fusion(bf16[2048,4096]{1,0:T(8,128)(2,1)} %collective-permute-done.4, s32[2048]{0:T(1024)S(1)} %broadcast_clamp_fusion.1), kind=kCustom, calls=%fused_computation.2 | custom fusion | bytes 33562624 | tf_op jit(solution)/shard_map/gather | solution.py:251
  111.8 233.3 %ffn.4 = bf16[2048,4096]{1,0:T(8,128)(2,1)} custom-call(s32[2]{0:T(128)} %get-tuple-element.481.blk.ex, s32[2]{0:T(128)} %compare_select_fusion.25.sub, s32[2]{0:T(128)} %get-tuple-element.481.blk.ex, bf16[2048,4096]{1,0:T(8,128)(2,1)} %gather_fusion.2, bf16[2,4096,6400]{2,1,0:T(8,128)(2,1)} %w1_ref.7, bf16[2,4096,6400]{2,1,0:T(8,128)(2,1)} %w3_ref.7, ...), custom_call_target="tpu_custom_call" | custom-call | flops 161061273600 | bytes 314572800 | tf_op jit(solution)/shard_map/ffn/pallas_call | solution.py:69
  345.8 61.9 %while.35 = (s32[]{:T(128)}, bf16[4096,4096]{1,0:T(8,128)(2,1)}, s32[]{:T(128)}, s32[]{:T(128)}, s32[4096]{0:T(1024)S(1)}, /*index=5*/bf16[4096,4096]{1,0:T(8,12...) while((s32[]{:T(128)}, bf16[4096,4096]{1,0:T(8,128)(2,1)}, s32[]{:T(128)}, ...), condition=%wide.region_54.55_spmd, body=%wide.region_53.54_spmd.sunk | while | flops 1803 | bytes 8397029 | solution.py:140
  357.4 5.9 gather_fusion
  363.4 1.5 constant_dynamic-update-slice_fusion.9
  366.8 20.3 %gather_fusion = bf16[256,4096]{1,0:T(8,128)(2,1)S(1)} fusion(bf16[4096,4096]{1,0:T(8,128)(2,1)} %get-tuple-element.853, s32[1024]{0:T(1024)S(1)} %pad_clamp_fusion.4), kind=kCustom, calls=%fused_computation.clone.1 | custom fusion | bytes 4195328 | tf_op jit(solution)/shard_map/while/body/gather | solution.py:137
  387.2 1.4 constant_dynamic-update-slice_fusion.9
  390.5 5.9 gather_fusion
  396.4 1.5 constant_dynamic-update-slice_fusion.9
  399.9 5.9 gather_fusion
  405.7 1.4 constant_dynamic-update-slice_fusion.9
  407.7 199.0 %ffn.5 = bf16[5120,4096]{1,0:T(8,128)(2,1)} custom-call(s32[4]{0:T(128)} %get-tuple-element.489.blk, s32[4]{0:T(128)} %compare_select_fusion.26.sub, s32[4]{0:T(128)} %get-tuple-element.484.ex, bf16[4096,4096]{1,0:T(8,128)(2,1)} %get-tuple-element.461.x_ref, bf16[2,4096,6400]{2,1,0:T(8,128)(2,1)} %w1_ref.7, bf16[2,4096,6400]{2,1,0:T(8,128)(2,1)} %w3_ref.7, ...), custom_call_target="tpu_custom_call" | custom-call | flops 161061273600 | bytes 314572800 | tf_op jit(solution)/shard_map/ffn/pallas_call | solution.py:69
  606.8 8.0 constant_dynamic-slice_fusion.20
  614.8 6.7 pad_maximum_fusion.4
  621.5 113.5 %collective-permute-start.5 = (bf16[832,4096]{1,0:T(8,128)(2,1)}, bf16[832,4096]{1,0:T(8,128)(2,1)}, u32[]{:S(2)}, u32[]{:S(2)}) collective-permute-start(bf16[832,4096]{1,0:T(8,128)(2,1)} %pad_maximum_fusion.4), channel_id=1, source_target_pairs={{0,2},{1,3},{2,0},{3,1},{4,6},{5,7},{6,4},{7,5}} | collective-permute-start | bytes 20447240 | tf_op jit(solution)/shard_map/ppermute | solution.py:261
  735.0 3.2 pad_maximum_fusion.5
  738.2 5.2 collective-permute-start.6
  743.5 55.9 %while.36 = (s32[]{:T(128)}, bf16[4096,4096]{1,0:T(8,128)(2,1)}, s32[]{:T(128)}, s32[]{:T(128)S(1)}, s32[4096]{0:T(1024)S(1)}, /*index=5*/bf16[4096,4096]{1,0:T(...) while((s32[]{:T(128)}, bf16[4096,4096]{1,0:T(8,128)(2,1)}, s32[]{:T(128)}, ...), condition=%wide.region_56.57_spmd, body=%wide.region_55.56_spmd.sunk | while | flops 1803 | bytes 8397029 | solution.py:140
  744.7 5.9 gather_fusion.1
  750.6 1.5 constant_dynamic-update-slice_fusion.10
  752.8 12.2 gather_fusion.1
  765.1 1.5 constant_dynamic-update-slice_fusion.10
  767.4 5.9 gather_fusion.1
  773.2 1.5 constant_dynamic-update-slice_fusion.10
  775.5 5.9 gather_fusion.1
  781.4 1.5 constant_dynamic-update-slice_fusion.10
  783.7 13.6 gather_fusion.1
  797.2 1.5 constant_dynamic-update-slice_fusion.10
  799.4 226.4 %ffn.6 = bf16[5120,4096]{1,0:T(8,128)(2,1)} custom-call(s32[4]{0:T(128)} %get-tuple-element.487.blk, s32[4]{0:T(128)} %compare_select_fusion.27.sub, s32[4]{0:T(128)} %get-tuple-element.485.ex, bf16[4096,4096]{1,0:T(8,128)(2,1)} %get-tuple-element.463.x_ref, bf16[2,4096,6400]{2,1,0:T(8,128)(2,1)} %w1_ref.7, bf16[2,4096,6400]{2,1,0:T(8,128)(2,1)} %w3_ref.7, ...), custom_call_target="tpu_custom_call" | custom-call | flops 161061273600 | bytes 314572800 | tf_op jit(solution)/shard_map/ffn/pallas_call | solution.py:69
  1025.8 8.0 constant_dynamic-slice_fusion.16
  1033.8 6.7 pad_maximum_fusion.6
  1040.6 70.3 %collective-permute-start.8 = (bf16[832,4096]{1,0:T(8,128)(2,1)}, bf16[832,4096]{1,0:T(8,128)(2,1)}, u32[]{:S(2)}, u32[]{:S(2)}) collective-permute-start(bf16[832,4096]{1,0:T(8,128)(2,1)} %pad_maximum_fusion.6), channel_id=1, source_target_pairs={{0,2},{1,3},{2,0},{3,1},{4,6},{5,7},{6,4},{7,5}} | collective-permute-start | bytes 20447240 | tf_op jit(solution)/shard_map/ppermute | solution.py:261
  1110.8 3.2 pad_maximum_fusion.7
  1114.0 2.0 collective-permute-start.9
  1116.2 36.7 %gather_fusion.3 = bf16[2048,4096]{1,0:T(8,128)(2,1)} fusion(bf16[2048,4096]{1,0:T(8,128)(2,1)} %param.12, s32[2048]{0:T(1024)S(1)} %broadcast_clamp_fusion.2), kind=kCustom, calls=%fused_computation.3 | custom fusion | bytes 33562624 | tf_op jit(solution)/shard_map/gather | solution.py:263
  1152.9 293.1 %ffn.7 = bf16[12288,4096]{1,0:T(8,128)(2,1)} custom-call(s32[2]{0:T(128)} %get-tuple-element.483.blk.ex, s32[2]{0:T(128)} %compare_select_fusion.28.sub, s32[2]{0:T(128)} %get-tuple-element.483.blk.ex, bf16[2048,4096]{1,0:T(8,128)(2,1)} %gather_fusion.3, bf16[2,4096,6400]{2,1,0:T(8,128)(2,1)} %w1_ref.7, bf16[2,4096,6400]{2,1,0:T(8,128)(2,1)} %w3_ref.7, ...), custom_call_target="tpu_custom_call" | custom-call | flops 161061273600 | bytes 314572800 | tf_op jit(solution)/shard_map/ffn/pallas_call | solution.py:69
  1446.0 14.0 constant_dynamic-update-slice_fusion.6
  1460.0 6.6 constant_dynamic-update-slice_fusion.5
  1466.6 6.6 constant_dynamic-update-slice_fusion.4
  1473.2 6.5 constant_dynamic-update-slice_fusion.3
  1479.8 6.6 constant_dynamic-update-slice_fusion.2
  1487.1 132.2 %gather_fusion.4 = bf16[4096,4096]{1,0:T(8,128)(2,1)} fusion(bf16[12288,4096]{1,0:T(8,128)(2,1)} %get-tuple-element.467, s32[4096]{0:T(1024)S(1)} %copy-done.3), kind=kCustom, calls=%fused_computation.4 | custom fusion | bytes 67125248 | tf_op jit(solution)/shard_map/gather | solution.py:283
  1619.4 29.5 %fusion = bf16[2048,4096]{1,0:T(8,128)(2,1)} fusion(bf16[2,2048,4096]{2,1,0:T(8,128)(2,1)} %bitcast.162, f32[2,2048]{1,0:T(2,128)S(1)} %copy-done.2), kind=kLoop, calls=%fused_computation.24 | loop fusion | flops 41943040 | bytes 50348032 | tf_op jit(solution)/shard_map/reduce_sum | solution.py:284
  (188 shorter events, 26.4 us)
Async XLA Ops:
  6.5 339.3 %all-gather.5.cloned.1.call-start = ((), (), s32[]{:S(2)}) async-start(), calls=%async_computation | async-start | bytes 41943040 | tf_op jit(solution)/shard_map/all_gather | solution.py:164
  29.6 713.9 %all-gather.7.cloned.1.call-start = ((), (), s32[]{:S(2)}) async-start(), calls=%async_computation.1 | async-start | bytes 41943040 | tf_op jit(solution)/shard_map/all_gather | solution.py:164
  29.6 45.4 %collective-permute-start.4 = (bf16[2048,4096]{1,0:T(8,128)(2,1)}, bf16[2048,4096]{1,0:T(8,128)(2,1)}, u32[]{:S(2)}, u32[]{:S(2)}) collective-permute-start(bf16[2048,4096]{1,0:T(8,128)(2,1)} %param.12), channel_id=1, source_target_pairs={{0,1},{1,0},{2,3},{3,2},{4,5},{5,4},{6,7},{7,6}} | collective-permute-start | bytes 50331656 | tf_op jit(solution)/shard_map/ppermute | solution.py:165
  42.9 4.6 copy-start
  42.9 7.8 copy-start.1
  345.1 1101.0 %collective-permute-start.7 = (bf16[2048,4096]{1,0:T(8,128)(2,1)}, bf16[2048,4096]{1,0:T(8,128)(2,1)}, u32[]{:S(2)}, u32[]{:S(2)}) collective-permute-start(bf16[2048,4096]{1,0:T(8,128)(2,1)} %ffn.4), channel_id=1, source_target_pairs={{0,1},{1,0},{2,3},{3,2},{4,5},{5,4},{6,7},{7,6}} | collective-permute-start | bytes 50331656 | tf_op jit(solution)/shard_map/ppermute | solution.py:253
  621.5 494.5 %collective-permute-start.5 = (bf16[832,4096]{1,0:T(8,128)(2,1)}, bf16[832,4096]{1,0:T(8,128)(2,1)}, u32[]{:S(2)}, u32[]{:S(2)}) collective-permute-start(bf16[832,4096]{1,0:T(8,128)(2,1)} %pad_maximum_fusion.4), channel_id=1, source_target_pairs={{0,2},{1,3},{2,0},{3,1},{4,6},{5,7},{6,4},{7,5}} | collective-permute-start | bytes 20447240 | tf_op jit(solution)/shard_map/ppermute | solution.py:261
  735.0 8.5 copy-start.4
  735.0 8.5 copy-start.6
  738.2 377.9 %collective-permute-start.6 = (bf16[832,4096]{1,0:T(8,128)(2,1)}, bf16[832,4096]{1,0:T(8,128)(2,1)}, u32[]{:S(2)}, u32[]{:S(2)}) collective-permute-start(bf16[832,4096]{1,0:T(8,128)(2,1)} %pad_maximum_fusion.5), channel_id=1, source_target_pairs={{0,3},{1,2},{2,1},{3,0},{4,7},{5,6},{6,5},{7,4}} | collective-permute-start | bytes 20447240 | tf_op jit(solution)/shard_map/ppermute | solution.py:261
  1040.6 432.7 %collective-permute-start.8 = (bf16[832,4096]{1,0:T(8,128)(2,1)}, bf16[832,4096]{1,0:T(8,128)(2,1)}, u32[]{:S(2)}, u32[]{:S(2)}) collective-permute-start(bf16[832,4096]{1,0:T(8,128)(2,1)} %pad_maximum_fusion.6), channel_id=1, source_target_pairs={{0,2},{1,3},{2,0},{3,1},{4,6},{5,7},{6,4},{7,5}} | collective-permute-start | bytes 20447240 | tf_op jit(solution)/shard_map/ppermute | solution.py:261
  1110.8 5.3 copy-start.5
  1114.0 365.7 %collective-permute-start.9 = (bf16[832,4096]{1,0:T(8,128)(2,1)}, bf16[832,4096]{1,0:T(8,128)(2,1)}, u32[]{:S(2)}, u32[]{:S(2)}) collective-permute-start(bf16[832,4096]{1,0:T(8,128)(2,1)} %pad_maximum_fusion.7), channel_id=1, source_target_pairs={{0,3},{1,2},{2,1},{3,0},{4,7},{5,6},{6,5},{7,4}} | collective-permute-start | bytes 20447240 | tf_op jit(solution)/shard_map/ppermute | solution.py:261
  1486.4 0.7 copy-start.3
  1487.1 132.2 %copy-start.2 = (f32[2,2048]{1,0:T(2,128)S(1)}, f32[2,2048]{1,0:T(2,128)}, u32[]{:S(2)}) copy-start(f32[2,2048]{1,0:T(2,128)} %divide_bitcast_fusion) | copy-start | bytes 49156
Sparse Core Ops, SparseCore 0:
  29.7 199.0 all-gather.4
  230.3 199.3 all-gather.6

commit v2 on v1

v2 whole, which is shorter than its diff:
```python
import functools

import jax
import jax.numpy as jnp
from jax import lax
from jax.experimental import pallas as pl
from jax.experimental.pallas import tpu as pltpu
from jax.sharding import PartitionSpec as P

VMEM_BYTES = 67043328
LANES = 128
SB = 1024
GRAN = 128
UNIT = 512
TAILS = (128, 256, 384)
CHUNK = 256
WIN = 512
CWIN = 144
CAP = 416
MORE = 152
BN1 = 256
BN2 = 256


def _for_rows(count, fn):
    unit = UNIT // GRAN
    whole = lax.div(count, unit)

    def body(i, c):
        fn(pl.multiple_of(i * UNIT, UNIT), UNIT)
        return c

    lax.fori_loop(0, whole, body, 0)
    rest = count - whole * unit
    for tail in TAILS:
        @pl.when(rest == tail // GRAN)
        def _():
            fn(pl.multiple_of(whole * UNIT, UNIT), tail)


def _ffn_kernel(blk, sub, ex, live, x_hbm, w1, w3, w2, o_hbm, xb, hb, wu, wd, ob, xsem, s1, s3, sd, so):
    n1, n2 = w1.shape[2] // BN1, w2.shape[2] // BN2
    count_live = live[0]

    def x_copy(s, slot):
        rows = pl.ds(pl.multiple_of(blk[s] * SB, SB), SB)
        return pltpu.make_async_copy(x_hbm.at[rows, :], xb.at[slot], xsem.at[slot])

    def up_copies(s, t, slot):
        cols = pl.ds(pl.multiple_of(t * BN1, BN1), BN1)
        return (pltpu.make_async_copy(w1.at[ex[s], :, cols], wu.at[slot, 0], s1.at[slot]),
                pltpu.make_async_copy(w3.at[ex[s], :, cols], wu.at[slot, 1], s3.at[slot]))

    def down_copy(s, t, slot):
        cols = pl.ds(pl.multiple_of(t * BN2, BN2), BN2)
        return pltpu.make_async_copy(w2.at[ex[s], :, cols], wd.at[slot], sd.at[slot])

    def out_copy(s, t, slot):
        rows = pl.ds(pl.multiple_of(blk[s] * SB, SB), SB)
        cols = pl.ds(pl.multiple_of(t * BN2, BN2), BN2)
        return pltpu.make_async_copy(ob.at[slot], o_hbm.at[rows, cols], so.at[slot])

    @pl.when(count_live > 0)
    def _():
        x_copy(0, 0).start()
        for c in up_copies(0, 0, 0):
            c.start()

    def superblock(s, carry):
        count = sub[s]
        side = s & 1
        down_copy(s, 0, 0).start()

        @pl.when(s + 1 < count_live)
        def _():
            x_copy(s + 1, 1 - side).start()
        x_copy(s, side).wait()

        def up_step(t, carry):
            slot = (s * n1 + t) & 1
            for c in up_copies(s, t, slot):
                c.wait()
            end = t == n1 - 1
            ns, nt = jnp.where(end, s + 1, s), jnp.where(end, 0, t + 1)

            @pl.when(ns < count_live)
            def _():
                for c in up_copies(ns, nt, 1 - slot):
                    c.start()
            col = pl.multiple_of(t * BN1, BN1)

            def up(r, m):
                x = xb[side, pl.ds(r, m), :]
                a = jnp.dot(x, wu[slot, 0], preferred_element_type=jnp.float32)
                b = jnp.dot(x, wu[slot, 1], preferred_element_type=jnp.float32)
                hb[pl.ds(r, m), pl.ds(col, BN1)] = (a * jax.nn.sigmoid(a) * b).astype(hb.dtype)
            _for_rows(count, up)
            return carry

        lax.fori_loop(0, n1, up_step, 0)

        def down_step(t, carry):
            slot = t & 1
            down_copy(s, t, slot).wait()

            @pl.when(t + 1 < n2)
            def _():
                down_copy(s, t + 1, 1 - slot).start()

            @pl.when(t >= 2)
            def _():
                out_copy(s, t - 2, slot).wait()

            def down(r, m):
                o = jnp.dot(hb[pl.ds(r, m), :], wd[slot], preferred_element_type=jnp.float32)
                ob[slot, pl.ds(r, m), :] = o.astype(ob.dtype)
            _for_rows(count, down)
            out_copy(s, t, slot).start()
            return carry

        lax.fori_loop(0, n2, down_step, 0)
        out_copy(s, n2 - 2, 0).wait()
        out_copy(s, n2 - 1, 1).wait()
        return carry

    lax.fori_loop(0, count_live, superblock, 0)


def _ffn(xs, w1, w3, w2, meta, rows_out, rows_hint):
    d, f = w1.shape[1], w1.shape[2]
    smem = pl.BlockSpec(memory_space=pltpu.SMEM)
    hbm = pl.BlockSpec(memory_space=pl.ANY)
    two = pltpu.SemaphoreType.DMA((2,))
    return pl.pallas_call(
        _ffn_kernel,
        out_shape=jax.ShapeDtypeStruct((rows_out, d), xs.dtype),
        in_specs=[smem] * 4 + [hbm] * 4,
        out_specs=hbm,
        scratch_shapes=[
            pltpu.VMEM((2, SB, d), xs.dtype), pltpu.VMEM((SB, f), xs.dtype), pltpu.VMEM((2, 2, d, BN1), xs.dtype),
            pltpu.VMEM((2, f, BN2), xs.dtype), pltpu.VMEM((2, SB, BN2), xs.dtype), two, two, two, two, two],
        compiler_params=pltpu.CompilerParams(vmem_limit_bytes=VMEM_BYTES),
        cost_estimate=pl.CostEstimate(
            flops=6 * rows_hint * d * f, bytes_accessed=12 * d * f, transcendentals=rows_hint * f),
        name="ffn",
    )(*meta, xs, w1, w3, w2)


def _pad8(n):
    return (n + 7) & ~7


def _row_list(incl, off, end, rows):
    c = incl.shape[0]
    r = lax.broadcasted_iota(jnp.int32, (rows, 1), 0)
    chunk = jnp.sum((end[None, :] <= r).astype(jnp.int32), axis=1, keepdims=True)
    hot = chunk == jnp.arange(c, dtype=jnp.int32)[None, :]
    start = jnp.sum(jnp.where(hot, off[None, :], 0), axis=1, keepdims=True)
    cum = jnp.dot(hot.astype(jnp.bfloat16), incl.astype(jnp.bfloat16), preferred_element_type=jnp.float32)
    lane = jnp.sum((cum <= (r - start).astype(jnp.float32)).astype(jnp.int32), axis=1, keepdims=True)
    return jnp.minimum(chunk * LANES + lane, c * LANES - 1)


def _blocks(counts, per, size):
    epd = counts.shape[0]
    i = jnp.arange(epd * per, dtype=jnp.int32)
    n = jnp.broadcast_to(counts[:, None], (epd, per)).reshape(-1)
    rows = jnp.clip(n - lax.rem(i, per) * size, 0, size)
    live = rows > 0
    slot = jnp.sum((live[None, :] & (i[None, :] < i[:, None])).astype(jnp.int32), axis=1)
    live_n = jnp.sum(live.astype(jnp.int32))
    put = (slot[None, :] == jnp.minimum(i, live_n - 1)[:, None]) & live[None, :]
    pick = lambda v: jnp.sum(jnp.where(put, v[None, :], 0), axis=1).astype(jnp.int32)
    return pick(i), pick(rows), pick(lax.div(i, per)), live_n[None]


def _meta(counts, per):
    blk, rows, ex, live = _blocks(counts, per, SB)
    return blk, lax.div(rows + GRAN - 1, GRAN), ex, live


def _gather_kernel(src, blk, first, last, live, list_ref, x_ref, o_ref, acc):
    i = pl.program_id(0)

    @pl.when(i < live[0])
    def _():
        lst = list_ref[...]
        acc[...] = jnp.zeros_like(acc)

        def window(w, c):
            lo = pl.multiple_of(w * WIN, WIN)
            lane = lax.broadcasted_iota(jnp.int32, (CHUNK, WIN), 1) + lo
            hot = jnp.where(lst == lane, 1.0, 0.0).astype(x_ref.dtype)
            acc[...] += jnp.dot(hot, x_ref[pl.ds(lo, WIN), :], preferred_element_type=jnp.float32)
            return c

        lax.fori_loop(lax.div(first[i], WIN), lax.div(last[i], WIN) + 1, window, 0)
        o_ref[...] = acc[...].astype(o_ref.dtype)


def _gather(x, src, tokens, lists, counts):
    rows, d = lists.shape[0], x.shape[1]
    per = rows // CHUNK // counts.shape[0]
    blk, cnt, _, live = _blocks(counts, per, CHUNK)
    table = lists.reshape(rows // CHUNK, CHUNK)
    at = blk[:, None] == jnp.arange(rows // CHUNK, dtype=jnp.int32)[None, :]
    lo = jnp.sum(jnp.where(at, table[:, 0][None, :], 0), axis=1)
    lane = jnp.arange(CHUNK, dtype=jnp.int32)[None, :]
    full = jnp.clip(jnp.broadcast_to(counts[:, None], (counts.shape[0], per)).reshape(-1)
                    - lax.rem(jnp.arange(rows // CHUNK, dtype=jnp.int32), per) * CHUNK, 0, CHUNK)
    top = jnp.max(jnp.where(lane < full[:, None], table, 0), axis=1)
    hi = jnp.sum(jnp.where(at, top[None, :], 0), axis=1)
    return pl.pallas_call(
        _gather_kernel,
        out_shape=jax.ShapeDtypeStruct((rows, d), x.dtype),
        grid_spec=pltpu.PrefetchScalarGridSpec(
            num_scalar_prefetch=5,
            grid=(rows // CHUNK,),
            in_specs=[pl.BlockSpec((CHUNK, 1), lambda i, src, blk, lo, hi, live: (blk[i], 0)),
                      pl.BlockSpec((tokens, d), lambda i, src, blk, lo, hi, live: (src[0], 0))],
            out_specs=pl.BlockSpec((CHUNK, d), lambda i, src, blk, lo, hi, live: (blk[i], 0)),
            scratch_shapes=[pltpu.VMEM((CHUNK, d), jnp.float32)],
        ),
        compiler_params=pltpu.CompilerParams(vmem_limit_bytes=VMEM_BYTES, dimension_semantics=("arbitrary",)),
        cost_estimate=pl.CostEstimate(flops=6 * rows * WIN * d, bytes_accessed=4 * tokens * d, transcendentals=0),
        name="rows",
    )(src, blk, lo, hi, live, lists, x)


def _combine_kernel(lo, cnt, loc_ref, g_ref, own, sib, f00, f01, f10, f11, y_ref, win, sem):
    b, nb = pl.program_id(0), pl.num_programs(0)
    slots = loc_ref.shape[1]
    epd = slots // 4
    d = y_ref.shape[1]

    def copy(ref, stride, b, k, side):
        row = pl.multiple_of((k % epd) * stride + lo[b * slots + k], 16)
        return pltpu.make_async_copy(ref.at[pl.ds(row, CWIN), :], win.at[side, k], sem.at[side, k])

    def start(b, side):
        stride = own.shape[0] // epd
        for k in range(2 * epd):
            copy(own if k < epd else sib, stride, b, k, side).start()
        for h, pair in enumerate(((f00, f01), (f10, f11))):
            @pl.when((b >= nb // 2) == (h == 1))
            def _():
                for k in range(2 * epd, slots):
                    copy(pair[k // epd - 2], CAP, b, k, side).start()

    side = b & 1

    @pl.when(b == 0)
    def _():
        start(0, 0)

    @pl.when(b + 1 < nb)
    def _():
        start(b + 1, 1 - side)

    for k in range(slots):
        copy(own if k < 2 * epd else f00, 0, b, k, side).wait()

    row = lax.broadcasted_iota(jnp.int32, (LANES, CWIN), 1)
    hots = [jnp.where(loc_ref[:, k:k + 1] == row, 1.0, 0.0).astype(y_ref.dtype) for k in range(slots)]
    step = 512

    def columns(c, carry):
        cols = pl.ds(pl.multiple_of(c * step, step), step)
        y = jnp.zeros((LANES, step), jnp.float32)
        r = lax.broadcasted_iota(jnp.int32, (CWIN, step), 0)
        for k in range(slots):
            w = win[side, k, :, cols].astype(jnp.float32)
            w = jnp.where(r < cnt[b * slots + k], w, 0.0).astype(win.dtype)
            y += g_ref[:, k:k + 1] * jnp.dot(hots[k], w, preferred_element_type=jnp.float32)
        y_ref[:, cols] = y.astype(y_ref.dtype)
        return carry

    lax.fori_loop(0, d // step, columns, 0)


def _combine(lo, cnt, loc, gates, arrays, dtype):
    t, slots = loc.shape
    d = arrays[0].shape[1]
    hbm = pl.BlockSpec(memory_space=pl.ANY)
    return pl.pallas_call(
        _combine_kernel,
        out_shape=jax.ShapeDtypeStruct((t, d), dtype),
        grid_spec=pltpu.PrefetchScalarGridSpec(
            num_scalar_prefetch=2,
            grid=(t // LANES,),
            in_specs=[pl.BlockSpec((LANES, slots), lambda b, lo, cnt: (b, 0))] * 2 + [hbm] * 6,
            out_specs=pl.BlockSpec((LANES, d), lambda b, lo, cnt: (b, 0)),
            scratch_shapes=[pltpu.VMEM((2, slots, CWIN, d), dtype), pltpu.SemaphoreType.DMA((2, slots))],
        ),
        compiler_params=pltpu.CompilerParams(vmem_limit_bytes=VMEM_BYTES, dimension_semantics=("arbitrary",)),
        name="combine",
    )(lo, cnt, loc, gates, *arrays)


def solution(mesh):
    n = mesh.shape['expert']

    def local(x, idx, wr, w1, w3, w2):
        t, d = x.shape
        k = idx.shape[1]
        e_all = wr.shape[1]
        epd = w1.shape[0]
        cs = 2 * k * t // e_all
        half = t // 2
        nc = t // LANES
        hc = nc // 2
        me = lax.axis_index('expert')
        sib = me ^ 1
        far = (me ^ 2) & ~1
        i32 = jnp.int32

        idx_t = idx.T
        idx_g = lax.all_gather(idx_t, ('data', 'expert'))
        xg, idx_g = lax.optimization_barrier((x, idx_g))
        idx_all = lax.dynamic_slice_in_dim(idx_g, lax.axis_index('data') * n, n, axis=0)
        x_h = [lax.all_gather(xg[h * half:(h + 1) * half], 'expert', tiled=True) for h in range(2)]
        x_sib = lax.ppermute(x, 'expert', [(i, i + 1 - 2 * (i % 2)) for i in range(n)])

        ids = jnp.arange(e_all, dtype=i32)
        hit = jnp.any(idx_all[:, None, :, :] == ids[None, :, None, None], axis=2)
        hit = hit.reshape(n, e_all, nc, LANES)
        lane = jnp.arange(LANES, dtype=i32)
        tri = (lane[:, None] <= lane[None, :]).astype(jnp.bfloat16)
        incl = jnp.dot(hit.astype(jnp.bfloat16), tri, preferred_element_type=jnp.float32).astype(i32)
        tot = incl[..., LANES - 1]
        ch = jnp.arange(nc, dtype=i32)
        off = jnp.sum(jnp.where(ch[None, :] < ch[:, None], tot[:, :, None, :], 0), axis=3)
        n_h = jnp.stack([jnp.sum(tot[..., :hc], axis=-1), jnp.sum(tot[..., hc:], axis=-1)], axis=1)

        dev = jnp.arange(n, dtype=i32)
        e_dev = lax.div(ids, epd)
        own = e_dev == me
        far_e = (e_dev >> 1) != (me >> 1)
        extra = cs - CAP
        far_base = 2 * epd * cs
        over_base = far_base + 2 * 2 * epd * CAP
        buf_rows = -(-(over_base + 2 * 2 * epd * extra) // SB) * SB

        take1 = lambda a, i: lax.dynamic_index_in_dim(a, i, 0, keepdims=False)
        mine = lambda a: lax.dynamic_slice_in_dim(a, me * epd, epd, axis=1)

        my_off, my_incl = take1(off, me), take1(incl, me)
        my_hit = take1(hit, me).astype(i32)
        rank = (my_incl - my_hit + my_off[:, :, None]).reshape(e_all, t)
        my_n0 = take1(n_h, me)[0]
        second = (jnp.arange(t, dtype=i32) >= half)[None, :]
        cross = ((e_dev ^ me) & 1) == 1
        slot = cross.astype(i32) * epd + lax.rem(ids, epd)
        far_rank = rank - jnp.where(second, my_n0[:, None], 0)
        far_slot = second.astype(i32) * 2 * epd + slot[:, None]
        far_place = jnp.where(far_rank < CAP, far_base + far_slot * CAP + far_rank,
                              over_base + far_slot * extra + far_rank - CAP)
        near_place = jnp.where(own, lax.rem(ids, epd), epd + lax.rem(ids, epd))[:, None] * cs + rank
        place = jnp.where(far_e[:, None], far_place, near_place)
        pos = jnp.sum(jnp.where(idx_t[:, None, :] == ids[None, :, None], place[None], 0), axis=1)

        incl_l, off_l, tot_l = mine(incl), mine(off), mine(tot)
        n_hl = lax.dynamic_slice_in_dim(n_h, me * epd, epd, axis=2)

        def one_source(s):
            a, o, tt = take1(incl_l, s), take1(off_l, s), take1(tot_l, s)
            return jnp.concatenate([_row_list(a[e], o[e], o[e] + tt[e], cs) for e in range(epd)]), take1(n_hl, s).sum(axis=0)

        def far_half(h):
            sl = slice(h * hc, (h + 1) * hc)
            pick = lambda a: jnp.moveaxis(lax.dynamic_slice_in_dim(a, far, 2, axis=0)[:, :, sl], 0, 1)
            a, tt = pick(incl_l), pick(tot_l)
            cnt = lax.dynamic_slice_in_dim(n_hl, far, 2, axis=0)[:, h]
            o = pick(off_l) - (lax.dynamic_slice_in_dim(n_hl, far, 2, axis=0)[:, 0].T[:, :, None] if h else 0)
            p0 = _pad8(cnt[0])
            o = o + jnp.stack([jnp.zeros_like(p0), p0], axis=1)[:, :, None]
            o = o.reshape(epd, nc)
            end = jnp.concatenate([o[:, 1:], (p0 + cnt[1])[:, None]], axis=1)
            a = a.reshape(epd, nc, LANES)
            lst = jnp.concatenate([_row_list(a[e], o[e], end[e], 2 * cs) for e in range(epd)])
            return lst, p0 + cnt[1]

        l_own, c_own = one_source(me)
        l_sib, c_sib = one_source(sib)
        l_far, c_far = zip(far_half(0), far_half(1))

        logits = jnp.dot(x, wr, preferred_element_type=jnp.float32)
        g = jax.nn.softmax(jnp.sum(jnp.where(idx[:, :, None] == ids, logits[:, None, :], 0.0), axis=2), axis=-1)

        hint = t * k * n // e_all * epd // 4
        perm = {m: [(i, i ^ m) for i in range(n)] for m in (1, 2, 3)}

        hit_g = jnp.any(idx_g[:, None, :, :] == ids[:, None, None], axis=2)
        most = jnp.max(jnp.sum(hit_g.reshape(-1, 2, half).astype(i32), axis=2))
        steps = jnp.maximum(lax.div(most - CAP + MORE - 1, MORE), 0)

        def start_of(h, home, e):
            first = jnp.where((home & 1) == 1, _pad8(take1(n_hl, home & ~1)[h, e]), 0)
            return pl.multiple_of(e * 2 * cs + first, 8)

        def pack(o, h, m, lo, size):
            home = me ^ m
            return jnp.concatenate([lax.dynamic_slice(o, (start_of(h, home, e) + lo, 0), (size, d)) for e in range(epd)])

        def far_rows(o, h, m, lo, size):
            return lax.ppermute(pack(o, h, m, lo, size), 'expert', perm[m])

        zero = jnp.zeros((1,), i32)
        xs = _gather(x_sib, zero, t, l_sib, c_sib)
        o_sib = _ffn(xs, w1, w3, w2, _meta(c_sib, cs // SB), epd * cs, hint)
        r_sib = lax.ppermute(o_sib, 'expert', perm[1])
        out, o_far, r_far = [o_sib], [], []
        for h in range(2):
            lst, out = lax.optimization_barrier((l_far[h], out))
            xs = _gather(x_h[h], (far >> 1)[None], 2 * half, lst, c_far[h])
            last = _ffn(xs, w1, w3, w2, _meta(c_far[h], 2 * cs // SB), epd * 2 * cs + SB, hint)
            o_far.append(last)
            out = [pack(last, h, m, 0, CAP) for m in (2, 3)]
            r_far.append([lax.ppermute(o, 'expert', perm[m]) for o, m in zip(out, (2, 3))])
        lst, out, r_far[0] = lax.optimization_barrier((l_own, out, r_far[0]))
        xs = _gather(x, zero, t, lst, c_own)
        o_own = _ffn(xs, w1, w3, w2, _meta(c_own, cs // SB), epd * cs, hint)

        k8 = jnp.arange(e_all, dtype=i32)
        slot_e = (lax.div(k8, epd) ^ me) * epd + lax.rem(k8, epd)
        by_slot = lambda a: jnp.sum(jnp.where((slot_e[:, None] == ids[None, :])[:, :, None], a[None], 0), axis=1)
        is_far = (k8 >= 2 * epd)[:, None]
        chunk_h = (ch >= hc)[None, :]
        s_n = by_slot(take1(n_h, me).T)
        base = jnp.where(is_far & chunk_h, s_n[:, :1], 0)
        held = jnp.where(is_far, jnp.where(chunk_h, s_n[:, 1:], s_n[:, :1]), s_n[:, :1] + s_n[:, 1:])
        lo = jnp.minimum((by_slot(my_off) - base) & ~15, jnp.where(is_far, CAP, cs) - CWIN)
        s_rank = by_slot(rank).reshape(e_all, nc, LANES) - base[:, :, None] - lo[:, :, None]
        s_hit = by_slot(my_hit.reshape(e_all, t)).reshape(e_all, nc, LANES) > 0
        loc = jnp.where(s_hit, s_rank, -1).reshape(e_all, t).T
        gates = jnp.sum(jnp.where(idx[:, :, None] == slot_e, g[:, :, None], 0.0), axis=1)
        arrays = (o_own, r_sib, *r_far[0], *r_far[1])

        def fast(arrays):
            return _combine(lo.T.reshape(-1), (held - lo).T.reshape(-1), loc, gates, arrays, x.dtype)

        def slow(arrays):
            buf = jnp.concatenate(arrays + (jnp.zeros((buf_rows - over_base, d), x.dtype),))

            def more(step, buf):
                for h in range(2):
                    for i, m in enumerate((2, 3)):
                        first = CAP + step * MORE
                        got = far_rows(o_far[h], h, m, first, MORE)
                        for e in range(epd):
                            row = over_base + ((2 * h + i) * epd + e) * extra + first - CAP
                            buf = lax.dynamic_update_slice(buf, got[e * MORE:(e + 1) * MORE], (row, 0))
                return buf

            buf = lax.fori_loop(0, steps, more, buf)
            op = buf.at[pos.reshape(-1)].get(mode='promise_in_bounds').reshape(k, t, d)
            return jnp.sum(g.T[:, :, None] * op.astype(jnp.float32), axis=0).astype(x.dtype)

        return lax.cond(steps > 0, slow, fast, arrays)

    tok = P(('data', 'expert'), None)
    wsp = P('expert', None, None)
    return jax.shard_map(local, mesh=mesh, in_specs=(tok, tok, P(), wsp, wsp, wsp), out_specs=tok, check_vma=False)
```

time: 1670 us -> 1400 us (0.84)
  the two profiles are of different devices: /device:TPU:2 before, /device:TPU:0 now
where the time goes in v2:
time: 1400 us; the launch traced here: 1380 us
  Pallas kernels  1160 us (83%)
  other arithmetic  55.3 us (4%)
  local copies, waits for them, and re-layouts  55 us (4%)
  starting transfers between devices  51.4 us (4%)
  between operations  25.3 us (2%)
    pallas_call x4, Pallas kernels, _ffn(): pl.pallas_call(_ffn_kernel, out_shape=jax.ShapeDtypeStruct((rows_out, d),...  981 us
    pallas_call x4, Pallas kernels, _gather(): pl.pallas_call(_gather_kernel, out_shape=jax.ShapeDtypeStruct((rows, d),...  105 us
    pallas_call x1, Pallas kernels, _combine(): pl.pallas_call(_combine_kernel, out_shape=jax.ShapeDtypeStruct((t, d), dt...  70.2 us
    ppermute x1, starting transfers between devices, local(): r_sib = lax.ppermute(o_sib, 'expert', perm[1])  51.2 us
  transfers between devices with their start and end apart: 8, of which 1 were waited for; matrix products, arithmetic and copies ran while one was open for 7% of the time, Pallas kernels for 79%

profile of v2, /device:TPU:0, one launch (start us, length us, event | category | flops | bytes accessed | tf_op | source)
XLA Modules:
  0.0 1380.7 jit_solution(4267775722379855629)
XLA Ops:
  6.5 13.9 %all-gather.1 = s32[8,2,2048]{2,1,0:T(2,128)S(1)} all-gather(s32[1,2,2048]{2,1,0:T(2,128)} %bitcast.204), channel_id=2, replica_groups=mesh['data'=2,'expert'=4] {'data','expert'}, dimensions={0}, use_global_device_ids=true | all-gather | bytes 147456 | tf_op jit(solution)/shard_map/all_gather | solution.py:318
  20.5 11.7 fusion.106
  33.3 0.7 fusion.107
  34.4 0.8 fusion.74
  35.2 0.7 fusion.73
  36.6 0.7 fusion.72
  37.4 0.8 fusion.76
  38.9 0.7 fusion.70
  54.5 10.2 fusion.111
  70.6 1.4 copy.84.list_ref
  72.8 1.2 reduce_sum.703
  75.8 0.8 select_reduce_fusion.23.blk
  78.2 0.7 select_reduce_fusion.28
  80.9 0.9 select_reduce_fusion.32
  88.2 1.2 fusion.103
  90.7 0.7 fusion.34
  91.4 23.8 %rows.4.x_hbm = bf16[2048,4096]{1,0:T(8,128)(2,1)} custom-call(s32[1]{0:T(128)} %constant.712.clone.1.src, s32[8]{0:T(128)} %copy-done.28, s32[8]{0:T(128)} %get-tuple-element.934.first, s32[8]{0:T(128)} %get-tuple-element.933.last, s32[1]{0:T(128)} %bitcast.81.live, s32[2048,1]{1,0:T(8,128)} %copy.84.list_ref, bf16[2048,4096]{1,0:T(8,128)(2,1)} %collective-permute-done.4.x_ref), custom_call_target="tpu_custom_call" | custom-call | flops 25769803776 | bytes 33554432 | tf_op jit(solution)/shard_map/rows/pallas_call | solution.py:213
  115.2 183.1 %ffn.4 = bf16[2048,4096]{1,0:T(8,128)(2,1)} custom-call(s32[2]{0:T(128)} %get-tuple-element.922.blk.ex, s32[2]{0:T(128)} %compare_select_fusion.3.sub, s32[2]{0:T(128)} %get-tuple-element.922.blk.ex, s32[1]{0:T(128)} %bitcast.74.live, bf16[2048,4096]{1,0:T(8,128)(2,1)} %rows.4.x_hbm, bf16[2,4096,6400]{2,1,0:T(8,128)(2,1)} %w1.7, bf16[2,4096,6400]{2,1,0:T(8,128)(2,1)} %w3.7, ...), custom_call_target="tpu_custom_call" | custom-call | flops 161061273600 | bytes 314572800 | tf_op jit(solution)/shard_map/ffn/pallas_call | solution.py:134
  298.3 2.7 copy.85.list_ref
  301.0 1.4 reduce.55
  302.4 51.2 %collective-permute-start.7 = (bf16[2048,4096]{1,0:T(8,128)(2,1)}, bf16[2048,4096]{1,0:T(8,128)(2,1)}, u32[]{:S(2)}, u32[]{:S(2)}) collective-permute-start(bf16[2048,4096]{1,0:T(8,128)(2,1)} %ffn.4), channel_id=1, source_target_pairs={{0,1},{1,0},{2,3},{3,2},{4,5},{5,4},{6,7},{7,6}} | collective-permute-start | bytes 50331656 | tf_op jit(solution)/shard_map/ppermute | solution.py:411
  353.7 0.8 select_reduce_fusion.16
  354.6 1.4 select_reduce_fusion.20
  355.9 27.8 %rows.5.x_hbm = bf16[4096,4096]{1,0:T(8,128)(2,1)} custom-call(s32[1]{0:T(128)} %bitcast.49.src, s32[16]{0:T(128)} %select_reduce_fusion.23.blk, s32[16]{0:T(128)} %get-tuple-element.932.first, s32[16]{0:T(128)} %get-tuple-element.931.last, s32[1]{0:T(128)} %bitcast.82.live, s32[4096,1]{1,0:T(8,128)} %copy.85.list_ref, ...), custom_call_target="tpu_custom_call" | custom-call | flops 51539607552 | bytes 33554432 | tf_op jit(solution)/shard_map/rows/pallas_call | solution.py:213
  383.7 282.6 %ffn.5 = bf16[5120,4096]{1,0:T(8,128)(2,1)} custom-call(s32[4]{0:T(128)} %get-tuple-element.940.blk, s32[4]{0:T(128)} %compare_select_fusion.5.sub, s32[4]{0:T(128)} %get-tuple-element.935.ex, s32[1]{0:T(128)} %bitcast.63.live, bf16[4096,4096]{1,0:T(8,128)(2,1)} %rows.5.x_hbm, bf16[2,4096,6400]{2,1,0:T(8,128)(2,1)} %w1.7, bf16[2,4096,6400]{2,1,0:T(8,128)(2,1)} %w3.7, ...), custom_call_target="tpu_custom_call" | custom-call | flops 161061273600 | bytes 314572800 | tf_op jit(solution)/shard_map/ffn/pallas_call | solution.py:134
  666.4 8.1 constant_dynamic-slice_fusion.17
  674.4 6.8 pad_maximum_fusion.5
  681.2 3.3 pad_maximum_fusion.4
  684.5 2.0 copy.86.list_ref
  687.6 0.8 select_reduce_fusion.18
  688.3 27.7 %rows.6.x_hbm = bf16[4096,4096]{1,0:T(8,128)(2,1)} custom-call(s32[1]{0:T(128)} %bitcast.49.src, s32[16]{0:T(128)} %select_reduce_fusion.24.blk, s32[16]{0:T(128)} %get-tuple-element.930.first, s32[16]{0:T(128)} %get-tuple-element.929.last, s32[1]{0:T(128)} %bitcast.89.live, s32[4096,1]{1,0:T(8,128)} %copy.86.list_ref, ...), custom_call_target="tpu_custom_call" | custom-call | flops 51539607552 | bytes 33554432 | tf_op jit(solution)/shard_map/rows/pallas_call | solution.py:213
  716.1 282.5 %ffn.6 = bf16[5120,4096]{1,0:T(8,128)(2,1)} custom-call(s32[4]{0:T(128)} %get-tuple-element.938.blk, s32[4]{0:T(128)} %compare_select_fusion.9.sub, s32[4]{0:T(128)} %get-tuple-element.936.ex, s32[1]{0:T(128)} %bitcast.48.live, bf16[4096,4096]{1,0:T(8,128)(2,1)} %rows.6.x_hbm, bf16[2,4096,6400]{2,1,0:T(8,128)(2,1)} %w1.7, bf16[2,4096,6400]{2,1,0:T(8,128)(2,1)} %w3.7, ...), custom_call_target="tpu_custom_call" | custom-call | flops 161061273600 | bytes 314572800 | tf_op jit(solution)/shard_map/ffn/pallas_call | solution.py:134
  998.6 8.0 constant_dynamic-slice_fusion.13
  1006.6 6.7 pad_maximum_fusion.7
  1013.3 3.3 pad_maximum_fusion.6
  1016.6 1.4 copy.87.list_ref
  1019.0 0.8 select_reduce_fusion.26
  1019.7 25.6 %rows.7.x_hbm = bf16[2048,4096]{1,0:T(8,128)(2,1)} custom-call(s32[1]{0:T(128)} %constant.712.clone.1.src, s32[8]{0:T(128)} %select_reduce_fusion.31.blk, s32[8]{0:T(128)} %get-tuple-element.928.first, s32[8]{0:T(128)} %get-tuple-element.927.last, s32[1]{0:T(128)} %bitcast.94.live, s32[2048,1]{1,0:T(8,128)} %copy.87.list_ref, bf16[2048,4096]{1,0:T(8,128)(2,1)} %x_ref.1), custom_call_target="tpu_custom_call" | custom-call | flops 25769803776 | bytes 33554432 | tf_op jit(solution)/shard_map/rows/pallas_call | solution.py:213
  1045.3 233.0 %ffn.7 = bf16[2048,4096]{1,0:T(8,128)(2,1)} custom-call(s32[2]{0:T(128)} %get-tuple-element.924.blk.ex, s32[2]{0:T(128)} %compare_select_fusion.15.sub, s32[2]{0:T(128)} %get-tuple-element.924.blk.ex, s32[1]{0:T(128)} %bitcast.40.live, bf16[2048,4096]{1,0:T(8,128)(2,1)} %rows.7.x_hbm, bf16[2,4096,6400]{2,1,0:T(8,128)(2,1)} %w1.7, bf16[2,4096,6400]{2,1,0:T(8,128)(2,1)} %w3.7, ...), custom_call_target="tpu_custom_call" | custom-call | flops 161061273600 | bytes 314572800 | tf_op jit(solution)/shard_map/ffn/pallas_call | solution.py:134
  1278.3 9.8 collective-permute-done.8
  1290.1 0.7 eq.201
  1290.9 1.4 add.1131
  1295.1 78.4 %conditional.1 = (bf16[2048,4096]{1,0:T(8,128)(2,1)}) conditional(s32[]{:T(128)} %convert_element_type.258, (pred[8,16]{1,0:T(8,128)(4,1)S(1)}, pred[8,16]{1,0:T(8,128)(4,1)S(1)}, s32[8,16]{1,0:T(8,128)S(1)}, s32[8,16]{1,0:T(8,128)}, s32[8]{0:T(128)}, /*index=5*/s32[8,2]{0,1:T(2,128)}, pred[8,16]{1,0:T(8,128)(4,1)S(1)}, s32[8,1]{0,1:T(1,128)}, ...), branch_computations={%region_82.84_spmd, %region_84.89_spmd} | conditional | flops 62267616 | bytes 380502720 | solution.py:459
  1295.9 0.8 copy.91
  1298.9 0.8 exponential_divide_fusion
  1299.8 1.3 copy.74.g_ref
  1301.1 2.2 copy.94.loc_ref
  1303.3 70.2 %combine.1 = bf16[2048,4096]{1,0:T(8,128)(2,1)} custom-call(s32[128]{0:T(128)} %reshape.1251.lo, s32[128]{0:T(128)} %reshape.1252.cnt, s32[2048,8]{1,0:T(8,128)} %copy.94.loc_ref, f32[2048,8]{1,0:T(8,128)} %copy.74.g_ref, bf16[2048,4096]{1,0:T(8,128)(2,1)} %get-tuple-element.668.own, bf16[2048,4096]{1,0:T(8,128)(2,1)} %get-tuple-element.669.sib, ...), custom_call_target="tpu_custom_call" | custom-call | tf_op jit(solution)/shard_map/cond/branch_0_fun/combine/pallas_call | solution.py:285
  (245 shorter events, 36.5 us)
Async XLA Ops:
  6.5 349.4 %all-gather.5.cloned.1.call-start = ((), (), s32[]{:S(2)}) async-start(), calls=%async_computation | async-start | bytes 41943040 | tf_op jit(solution)/shard_map/all_gather | solution.py:321
  32.2 22.2 %copy-start.15 = (bf16[4096,8]{0,1:T(8,128)(2,1)S(1)}, bf16[4096,8]{0,1:T(8,128)(2,1)}, u32[]{:S(2)}) copy-start(bf16[4096,8]{0,1:T(8,128)(2,1)} %param.12) | copy-start | bytes 196612
  32.2 656.1 %all-gather.7.cloned.1.call-start = ((), (), s32[]{:S(2)}) async-start(), calls=%async_computation.1 | async-start | bytes 41943040 | tf_op jit(solution)/shard_map/all_gather | solution.py:321
  32.3 59.1 %collective-permute-start.4 = (bf16[2048,4096]{1,0:T(8,128)(2,1)}, bf16[2048,4096]{1,0:T(8,128)(2,1)}, u32[]{:S(2)}, u32[]{:S(2)}) collective-permute-start(bf16[2048,4096]{1,0:T(8,128)(2,1)} %x_ref.1), channel_id=1, source_target_pairs={{0,1},{1,0},{2,3},{3,2},{4,5},{5,4},{6,7},{7,6}} | collective-permute-start | bytes 50331656 | tf_op jit(solution)/shard_map/ppermute | solution.py:322
  42.8 22.7 %copy-start.31 = (pred[16]{0:T(512)(128)(4,1)}, pred[16]{0:T(512)(128)(4,1)S(1)}, u32[]{:S(2)}) copy-start(pred[16]{0:T(512)(128)(4,1)S(1)} %iota_compare_fusion.41) | copy-start | bytes 52
  49.2 16.3 %copy-start.32 = (pred[8]{0:T(512)(128)(4,1)}, pred[8]{0:T(512)(128)(4,1)S(1)}, u32[]{:S(2)}) copy-start(pred[8]{0:T(512)(128)(4,1)S(1)} %iota_compare_fusion.42) | copy-start | bytes 28
  49.3 16.2 %copy-start.22 = (s32[8]{0:T(128)}, s32[8]{0:T(128)S(1)}, u32[]{:S(2)}) copy-start(s32[8]{0:T(128)S(1)} %select_add_fusion) | copy-start | bytes 100
  49.4 15.3 %copy-start.19 = (s32[1,2,8]{2,0,1:T(1,128)}, s32[1,2,8]{2,0,1:T(1,128)S(1)}, u32[]{:S(2)}) copy-start(s32[1,2,8]{2,0,1:T(1,128)S(1)} %fusion.83) | copy-start | bytes 196
  54.3 10.6 copy-start.21
  54.5 11.0 copy-start.17
  54.5 10.2 copy-start.3
  64.8 23.5 %copy-start.6 = (f32[2048,2]{0,1:T(2,128)}, f32[2048,2]{0,1:T(2,128)S(1)}, u32[]{:S(2)}) copy-start(f32[2048,2]{0,1:T(2,128)S(1)} %select_reduce_fusion.9) | copy-start | bytes 49156
  65.5 6.8 copy-start.23
  70.6 20.8 %copy-start.14 = (s32[8,16]{0,1:T(8,128)}, s32[8,16]{0,1:T(8,128)S(1)}, u32[]{:S(2)}) copy-start(s32[8,16]{0,1:T(8,128)S(1)} %copy.77) | copy-start | bytes 1540
  75.5 15.9 %copy-start.12 = (f32[2048]{0:T(1024)}, f32[2048]{0:T(1024)S(1)}, u32[]{:S(2)}) copy-start(f32[2048]{0:T(1024)S(1)} %reduce_max.55) | copy-start | bytes 24580
  75.8 6.2 copy-start.28
  80.3 3.9 copy-start
  84.3 0.6 copy-start.8
  302.4 976.0 %collective-permute-start.7 = (bf16[2048,4096]{1,0:T(8,128)(2,1)}, bf16[2048,4096]{1,0:T(8,128)(2,1)}, u32[]{:S(2)}, u32[]{:S(2)}) collective-permute-start(bf16[2048,4096]{1,0:T(8,128)(2,1)} %ffn.4), channel_id=1, source_target_pairs={{0,1},{1,0},{2,3},{3,2},{4,5},{5,4},{6,7},{7,6}} | collective-permute-start | bytes 50331656 | tf_op jit(solution)/shard_map/ppermute | solution.py:411
  681.2 3.3 copy-start.7
  681.2 6.2 copy-start.25
  681.2 6.4 copy-start.27
  687.2 329.4 %collective-permute-start.6 = (bf16[832,4096]{1,0:T(8,128)(2,1)}, bf16[832,4096]{1,0:T(8,128)(2,1)}, u32[]{:S(2)}, u32[]{:S(2)}) collective-permute-start(bf16[832,4096]{1,0:T(8,128)(2,1)} %pad_maximum_fusion.5), channel_id=1, source_target_pairs={{0,3},{1,2},{2,1},{3,0},{4,7},{5,6},{6,5},{7,4}} | collective-permute-start | bytes 20447240 | tf_op jit(solution)/shard_map/ppermute | solution.py:419
  687.2 329.4 %collective-permute-start.5 = (bf16[832,4096]{1,0:T(8,128)(2,1)}, bf16[832,4096]{1,0:T(8,128)(2,1)}, u32[]{:S(2)}, u32[]{:S(2)}) collective-permute-start(bf16[832,4096]{1,0:T(8,128)(2,1)} %pad_maximum_fusion.4), channel_id=1, source_target_pairs={{0,2},{1,3},{2,0},{3,1},{4,6},{5,7},{6,4},{7,5}} | collective-permute-start | bytes 20447240 | tf_op jit(solution)/shard_map/ppermute | solution.py:419
  1013.3 265.0 %collective-permute-start.9 = (bf16[832,4096]{1,0:T(8,128)(2,1)}, bf16[832,4096]{1,0:T(8,128)(2,1)}, u32[]{:S(2)}, u32[]{:S(2)}) collective-permute-start(bf16[832,4096]{1,0:T(8,128)(2,1)} %pad_maximum_fusion.7), channel_id=1, source_target_pairs={{0,3},{1,2},{2,1},{3,0},{4,7},{5,6},{6,5},{7,4}} | collective-permute-start | bytes 20447240 | tf_op jit(solution)/shard_map/ppermute | solution.py:419
  1013.3 3.3 copy-start.10
  1013.3 5.4 copy-start.24
  1013.3 5.6 copy-start.26
  1016.6 271.6 %collective-permute-start.8 = (bf16[832,4096]{1,0:T(8,128)(2,1)}, bf16[832,4096]{1,0:T(8,128)(2,1)}, u32[]{:S(2)}, u32[]{:S(2)}) collective-permute-start(bf16[832,4096]{1,0:T(8,128)(2,1)} %pad_maximum_fusion.6), channel_id=1, source_target_pairs={{0,2},{1,3},{2,0},{3,1},{4,6},{5,7},{6,4},{7,5}} | collective-permute-start | bytes 20447240 | tf_op jit(solution)/shard_map/ppermute | solution.py:419
Sparse Core Ops, SparseCore 0:
  32.4 199.5 all-gather.4
  233.5 199.4 all-gather.6

commit v3 on v2

--- a/solution.py
+++ b/solution.py
@@ -20,6 +20,7 @@
 MORE = 152
 BN1 = 256
 BN2 = 256
+AHEAD = 2
 
 
 def _for_rows(count, fn):
@@ -63,13 +64,15 @@
     @pl.when(count_live > 0)
     def _():
         x_copy(0, 0).start()
-        for c in up_copies(0, 0, 0):
-            c.start()
+        for t in range(AHEAD):
+            for c in up_copies(0, t, t):
+                c.start()
 
     def superblock(s, carry):
         count = sub[s]
         side = s & 1
-        down_copy(s, 0, 0).start()
+        for t in range(AHEAD):
+            down_copy(s, t, lax.rem(s * n2 + t, AHEAD + 1)).start()
 
         @pl.when(s + 1 < count_live)
         def _():
@@ -77,15 +80,16 @@
         x_copy(s, side).wait()
 
         def up_step(t, carry):
-            slot = (s * n1 + t) & 1
+            step = s * n1 + t
+            slot = lax.rem(step, AHEAD + 1)
             for c in up_copies(s, t, slot):
                 c.wait()
-            end = t == n1 - 1
-            ns, nt = jnp.where(end, s + 1, s), jnp.where(end, 0, t + 1)
+            end = t >= n1 - AHEAD
+            ns, nt = jnp.where(end, s + 1, s), jnp.where(end, t + AHEAD - n1, t + AHEAD)
 
             @pl.when(ns < count_live)
             def _():
-                for c in up_copies(ns, nt, 1 - slot):
+                for c in up_copies(ns, nt, lax.rem(step + AHEAD, AHEAD + 1)):
                     c.start()
             col = pl.multiple_of(t * BN1, BN1)
 
@@ -101,18 +105,19 @@
 
         def down_step(t, carry):
             slot = t & 1
-            down_copy(s, t, slot).wait()
-
-            @pl.when(t + 1 < n2)
+            here = lax.rem(s * n2 + t, AHEAD + 1)
+            down_copy(s, t, here).wait()
+
+            @pl.when(t + AHEAD < n2)
             def _():
-                down_copy(s, t + 1, 1 - slot).start()
+                down_copy(s, t + AHEAD, lax.rem(s * n2 + t + AHEAD, AHEAD + 1)).start()
 
             @pl.when(t >= 2)
             def _():
                 out_copy(s, t - 2, slot).wait()
 
             def down(r, m):
-                o = jnp.dot(hb[pl.ds(r, m), :], wd[slot], preferred_element_type=jnp.float32)
+                o = jnp.dot(hb[pl.ds(r, m), :], wd[here], preferred_element_type=jnp.float32)
                 ob[slot, pl.ds(r, m), :] = o.astype(ob.dtype)
             _for_rows(count, down)
             out_copy(s, t, slot).start()
@@ -131,14 +136,15 @@
     smem = pl.BlockSpec(memory_space=pltpu.SMEM)
     hbm = pl.BlockSpec(memory_space=pl.ANY)
     two = pltpu.SemaphoreType.DMA((2,))
+    ring = pltpu.SemaphoreType.DMA((AHEAD + 1,))
     return pl.pallas_call(
         _ffn_kernel,
         out_shape=jax.ShapeDtypeStruct((rows_out, d), xs.dtype),
         in_specs=[smem] * 4 + [hbm] * 4,
         out_specs=hbm,
         scratch_shapes=[
-            pltpu.VMEM((2, SB, d), xs.dtype), pltpu.VMEM((SB, f), xs.dtype), pltpu.VMEM((2, 2, d, BN1), xs.dtype),
-            pltpu.VMEM((2, f, BN2), xs.dtype), pltpu.VMEM((2, SB, BN2), xs.dtype), two, two, two, two, two],
+            pltpu.VMEM((2, SB, d), xs.dtype), pltpu.VMEM((SB, f), xs.dtype), pltpu.VMEM((AHEAD + 1, 2, d, BN1), xs.dtype),
+            pltpu.VMEM((AHEAD + 1, f, BN2), xs.dtype), pltpu.VMEM((2, SB, BN2), xs.dtype), two, ring, ring, ring, two],
         compiler_params=pltpu.CompilerParams(vmem_limit_bytes=VMEM_BYTES),
         cost_estimate=pl.CostEstimate(
             flops=6 * rows_hint * d * f, bytes_accessed=12 * d * f, transcendentals=rows_hint * f),
@@ -347,18 +353,6 @@
         my_off, my_incl = take1(off, me), take1(incl, me)
         my_hit = take1(hit, me).astype(i32)
         rank = (my_incl - my_hit + my_off[:, :, None]).reshape(e_all, t)
-        my_n0 = take1(n_h, me)[0]
-        second = (jnp.arange(t, dtype=i32) >= half)[None, :]
-        cross = ((e_dev ^ me) & 1) == 1
-        slot = cross.astype(i32) * epd + lax.rem(ids, epd)
-        far_rank = rank - jnp.where(second, my_n0[:, None], 0)
-        far_slot = second.astype(i32) * 2 * epd + slot[:, None]
-        far_place = jnp.where(far_rank < CAP, far_base + far_slot * CAP + far_rank,
-                              over_base + far_slot * extra + far_rank - CAP)
-        near_place = jnp.where(own, lax.rem(ids, epd), epd + lax.rem(ids, epd))[:, None] * cs + rank
-        place = jnp.where(far_e[:, None], far_place, near_place)
-        pos = jnp.sum(jnp.where(idx_t[:, None, :] == ids[None, :, None], place[None], 0), axis=1)
-
         incl_l, off_l, tot_l = mine(incl), mine(off), mine(tot)
         n_hl = lax.dynamic_slice_in_dim(n_h, me * epd, epd, axis=2)
 
@@ -408,7 +402,6 @@
         zero = jnp.zeros((1,), i32)
         xs = _gather(x_sib, zero, t, l_sib, c_sib)
         o_sib = _ffn(xs, w1, w3, w2, _meta(c_sib, cs // SB), epd * cs, hint)
-        r_sib = lax.ppermute(o_sib, 'expert', perm[1])
         out, o_far, r_far = [o_sib], [], []
         for h in range(2):
             lst, out = lax.optimization_barrier((l_far[h], out))
@@ -417,7 +410,8 @@
             o_far.append(last)
             out = [pack(last, h, m, 0, CAP) for m in (2, 3)]
             r_far.append([lax.ppermute(o, 'expert', perm[m]) for o, m in zip(out, (2, 3))])
-        lst, out, r_far[0] = lax.optimization_barrier((l_own, out, r_far[0]))
+        lst, out, r_far[0], o_home = lax.optimization_barrier((l_own, out, r_far[0], o_sib))
+        r_sib = lax.ppermute(o_home, 'expert', perm[1])
         xs = _gather(x, zero, t, lst, c_own)
         o_own = _ffn(xs, w1, w3, w2, _meta(c_own, cs // SB), epd * cs, hint)
 
@@ -440,6 +434,17 @@
             return _combine(lo.T.reshape(-1), (held - lo).T.reshape(-1), loc, gates, arrays, x.dtype)
 
         def slow(arrays):
+            my_n0 = take1(n_h, me)[0]
+            second = (jnp.arange(t, dtype=i32) >= half)[None, :]
+            cross = ((e_dev ^ me) & 1) == 1
+            slot = cross.astype(i32) * epd + lax.rem(ids, epd)
+            far_rank = rank - jnp.where(second, my_n0[:, None], 0)
+            far_slot = second.astype(i32) * 2 * epd + slot[:, None]
+            far_place = jnp.where(far_rank < CAP, far_base + far_slot * CAP + far_rank,
+                                  over_base + far_slot * extra + far_rank - CAP)
+            near_place = jnp.where(own, lax.rem(ids, epd), epd + lax.rem(ids, epd))[:, None] * cs + rank
+            place = jnp.where(far_e[:, None], far_place, near_place)
+            pos = jnp.sum(jnp.where(idx_t[:, None, :] == ids[None, :, None], place[None], 0), axis=1)
             buf = jnp.concatenate(arrays + (jnp.zeros((buf_rows - over_base, d), x.dtype),))
 
             def more(step, buf):

time: 1400 us -> 1380 us (0.986)
  starting transfers between devices: 51.4 us -> 5.05 us
  Pallas kernels: 1160 us -> 1200 us
    ppermute x1, starting transfers between devices: 51.2 us -> 0.9 us  [local(): r_sib = lax.ppermute(o_home, 'expert', perm[1])]
    pallas_call x4, Pallas kernels: 981 us -> 1020 us  [_ffn(): pl.pallas_call(_ffn_kernel, out_shape=jax.ShapeDtypeStruct((rows_out, d),...]
  transfers between devices with their start and end apart: 8 -> 8, of which waited for: 1 -> 1; matrix products, arithmetic and copies ran while one was open for 7% -> 7% of each run, Pallas kernels for 79% -> 82%
where the time goes in v3:
time: 1380 us; the launch traced here: 1370 us
  Pallas kernels  1200 us (87%)
  other arithmetic  56.1 us (4%)
  local copies, waits for them, and re-layouts  53.4 us (4%)
  between operations  25.1 us (2%)
  blocking collectives  13.9 us (1%)
    pallas_call x4, Pallas kernels, _ffn(): pl.pallas_call(_ffn_kernel, out_shape=jax.ShapeDtypeStruct((rows_out, d),...  1020 us
    pallas_call x4, Pallas kernels, _gather(): pl.pallas_call(_gather_kernel, out_shape=jax.ShapeDtypeStruct((rows, d),...  109 us
    pallas_call x1, Pallas kernels, _combine(): pl.pallas_call(_combine_kernel, out_shape=jax.ShapeDtypeStruct((t, d), dt...  70.2 us
  transfers between devices with their start and end apart: 8, of which 1 were waited for; matrix products, arithmetic and copies ran while one was open for 7% of the time, Pallas kernels for 82%

profile of v3, /device:TPU:0, one launch (start us, length us, event | category | flops | bytes accessed | tf_op | source)
XLA Modules:
  0.0 1374.7 jit_solution(7178970850212593912)
XLA Ops:
  6.5 13.9 %all-gather.1 = s32[8,2,2048]{2,1,0:T(2,128)S(1)} all-gather(s32[1,2,2048]{2,1,0:T(2,128)} %bitcast.199), channel_id=2, replica_groups=mesh['data'=2,'expert'=4] {'data','expert'}, dimensions={0}, use_global_device_ids=true | all-gather | bytes 147456 | tf_op jit(solution)/shard_map/all_gather | solution.py:324
  20.5 11.7 fusion.109
  34.4 0.7 fusion.79
  37.2 0.8 fusion.74
  38.0 0.7 fusion.75
  54.9 10.2 fusion.114
  70.8 1.4 copy.72.list_ref
  73.0 1.2 reduce_sum.702
  77.3 0.8 select_reduce_fusion.31.blk
  79.0 0.8 fusion.69
  79.7 0.7 fusion.68
  81.1 0.8 select_reduce_fusion.32
  87.6 0.8 pad_add_fusion.2
  88.4 1.2 fusion.106
  91.6 27.4 %rows.4.x_hbm = bf16[2048,4096]{1,0:T(8,128)(2,1)} custom-call(s32[1]{0:T(128)} %constant.712.clone.1.src, s32[8]{0:T(128)} %copy-done.25, s32[8]{0:T(128)} %get-tuple-element.822.first, s32[8]{0:T(128)} %get-tuple-element.821.last, s32[1]{0:T(128)} %bitcast.78.live, s32[2048,1]{1,0:T(8,128)} %copy.72.list_ref, bf16[2048,4096]{1,0:T(8,128)(2,1)} %collective-permute-done.4.x_ref), custom_call_target="tpu_custom_call" | custom-call | flops 25769803776 | bytes 33554432 | tf_op jit(solution)/shard_map/rows/pallas_call | solution.py:219
  119.0 282.6 %ffn.4 = bf16[2048,4096]{1,0:T(8,128)(2,1)} custom-call(s32[2]{0:T(128)} %get-tuple-element.810.blk.ex, s32[2]{0:T(128)} %compare_select_fusion.9.sub, s32[2]{0:T(128)} %get-tuple-element.810.blk.ex, s32[1]{0:T(128)} %bitcast.71.live, bf16[2048,4096]{1,0:T(8,128)(2,1)} %rows.4.x_hbm, bf16[2,4096,6400]{2,1,0:T(8,128)(2,1)} %w1.7, bf16[2,4096,6400]{2,1,0:T(8,128)(2,1)} %w3.7, ...), custom_call_target="tpu_custom_call" | custom-call | flops 161061273600 | bytes 314572800 | tf_op jit(solution)/shard_map/ffn/pallas_call | solution.py:140
  401.6 2.7 copy.73.list_ref
  404.3 1.4 reduce.55
  405.8 0.9 select_reduce_fusion.16
  406.7 1.3 select_reduce_fusion.20
  408.0 27.7 %rows.5.x_hbm = bf16[4096,4096]{1,0:T(8,128)(2,1)} custom-call(s32[1]{0:T(128)} %bitcast.46.src, s32[16]{0:T(128)} %select_reduce_fusion.23.blk, s32[16]{0:T(128)} %get-tuple-element.820.first, s32[16]{0:T(128)} %get-tuple-element.819.last, s32[1]{0:T(128)} %bitcast.79.live, s32[4096,1]{1,0:T(8,128)} %copy.73.list_ref, ...), custom_call_target="tpu_custom_call" | custom-call | flops 51539607552 | bytes 33554432 | tf_op jit(solution)/shard_map/rows/pallas_call | solution.py:219
  435.8 243.0 %ffn.5 = bf16[5120,4096]{1,0:T(8,128)(2,1)} custom-call(s32[4]{0:T(128)} %get-tuple-element.828.blk, s32[4]{0:T(128)} %compare_select_fusion.11.sub, s32[4]{0:T(128)} %get-tuple-element.823.ex, s32[1]{0:T(128)} %bitcast.60.live, bf16[4096,4096]{1,0:T(8,128)(2,1)} %rows.5.x_hbm, bf16[2,4096,6400]{2,1,0:T(8,128)(2,1)} %w1.7, bf16[2,4096,6400]{2,1,0:T(8,128)(2,1)} %w3.7, ...), custom_call_target="tpu_custom_call" | custom-call | flops 161061273600 | bytes 314572800 | tf_op jit(solution)/shard_map/ffn/pallas_call | solution.py:140
  678.8 8.1 constant_dynamic-slice_fusion.18
  686.9 6.7 pad_maximum_fusion.5
  693.6 3.3 pad_maximum_fusion.4
  696.9 2.0 copy.74.list_ref
  698.9 0.7 reduce.56
  700.8 26.0 %rows.6.x_hbm = bf16[4096,4096]{1,0:T(8,128)(2,1)} custom-call(s32[1]{0:T(128)} %bitcast.46.src, s32[16]{0:T(128)} %select_reduce_fusion.24.blk, s32[16]{0:T(128)} %get-tuple-element.818.first, s32[16]{0:T(128)} %get-tuple-element.817.last, s32[1]{0:T(128)} %bitcast.86.live, s32[4096,1]{1,0:T(8,128)} %copy.74.list_ref, ...), custom_call_target="tpu_custom_call" | custom-call | flops 51539607552 | bytes 33554432 | tf_op jit(solution)/shard_map/rows/pallas_call | solution.py:219
  726.8 215.6 %ffn.6 = bf16[5120,4096]{1,0:T(8,128)(2,1)} custom-call(s32[4]{0:T(128)} %get-tuple-element.826.blk, s32[4]{0:T(128)} %compare_select_fusion.15.sub, s32[4]{0:T(128)} %get-tuple-element.824.ex, s32[1]{0:T(128)} %bitcast.45.live, bf16[4096,4096]{1,0:T(8,128)(2,1)} %rows.6.x_hbm, bf16[2,4096,6400]{2,1,0:T(8,128)(2,1)} %w1.7, bf16[2,4096,6400]{2,1,0:T(8,128)(2,1)} %w3.7, ...), custom_call_target="tpu_custom_call" | custom-call | flops 161061273600 | bytes 314572800 | tf_op jit(solution)/shard_map/ffn/pallas_call | solution.py:140
  942.4 8.2 constant_dynamic-slice_fusion.14
  950.6 6.7 pad_maximum_fusion.7
  957.3 3.4 pad_maximum_fusion.6
  960.7 4.0 collective-permute-start.8
  964.7 5.0 collective-permute-done.5
  969.7 1.4 copy.75.list_ref
  972.1 0.9 collective-permute-start.7
  973.0 0.8 select_reduce_fusion.26
  973.8 27.4 %rows.7.x_hbm = bf16[2048,4096]{1,0:T(8,128)(2,1)} custom-call(s32[1]{0:T(128)} %constant.712.clone.1.src, s32[8]{0:T(128)} %select_reduce_fusion.31.blk, s32[8]{0:T(128)} %get-tuple-element.816.first, s32[8]{0:T(128)} %get-tuple-element.815.last, s32[1]{0:T(128)} %bitcast.91.live, s32[2048,1]{1,0:T(8,128)} %copy.75.list_ref, bf16[2048,4096]{1,0:T(8,128)(2,1)} %x_ref.1), custom_call_target="tpu_custom_call" | custom-call | flops 25769803776 | bytes 33554432 | tf_op jit(solution)/shard_map/rows/pallas_call | solution.py:219
  1001.2 282.6 %ffn.7 = bf16[2048,4096]{1,0:T(8,128)(2,1)} custom-call(s32[2]{0:T(128)} %get-tuple-element.812.blk.ex, s32[2]{0:T(128)} %compare_select_fusion.21.sub, s32[2]{0:T(128)} %get-tuple-element.812.blk.ex, s32[1]{0:T(128)} %bitcast.37.live, bf16[2048,4096]{1,0:T(8,128)(2,1)} %rows.7.x_hbm, bf16[2,4096,6400]{2,1,0:T(8,128)(2,1)} %w1.7, bf16[2,4096,6400]{2,1,0:T(8,128)(2,1)} %w3.7, ...), custom_call_target="tpu_custom_call" | custom-call | flops 161061273600 | bytes 314572800 | tf_op jit(solution)/shard_map/ffn/pallas_call | solution.py:140
  1283.8 1.4 add.1067
  1286.3 0.7 broadcast_in_dim.710
  1288.3 0.7 eq.193
  1289.1 78.4 %conditional.1 = (bf16[2048,4096]{1,0:T(8,128)(2,1)}) conditional(s32[]{:T(128)} %convert_element_type.251, (pred[8,16]{1,0:T(8,128)(4,1)S(1)}, pred[8,16]{1,0:T(8,128)(4,1)S(1)}, s32[8,16]{1,0:T(8,128)S(1)}, s32[8,16]{1,0:T(8,128)}, s32[8]{0:T(128)}, /*index=5*/s32[8,2]{0,1:T(2,128)}, pred[8,16]{1,0:T(8,128)(4,1)S(1)}, s32[8,1]{0,1:T(1,128)}, ...), branch_computations={%region_82.84_spmd, %region_84.89_spmd} | conditional | flops 62267736 | bytes 379797696 | solution.py:464
  1289.8 0.8 copy.79
  1292.9 0.8 exponential_divide_fusion
  1293.8 1.3 copy.62.g_ref
  1295.1 2.2 copy.82.loc_ref
  1297.3 70.2 %combine.1 = bf16[2048,4096]{1,0:T(8,128)(2,1)} custom-call(s32[128]{0:T(128)} %reshape.1065.lo, s32[128]{0:T(128)} %reshape.1066.cnt, s32[2048,8]{1,0:T(8,128)} %copy.82.loc_ref, f32[2048,8]{1,0:T(8,128)} %copy.62.g_ref, bf16[2048,4096]{1,0:T(8,128)(2,1)} %get-tuple-element.578.own, bf16[2048,4096]{1,0:T(8,128)(2,1)} %get-tuple-element.579.sib, ...), custom_call_target="tpu_custom_call" | custom-call | tf_op jit(solution)/shard_map/cond/branch_0_fun/combine/pallas_call | solution.py:291
  (241 shorter events, 36.1 us)
Async XLA Ops:
  6.5 401.5 %all-gather.5.cloned.1.call-start = ((), (), s32[]{:S(2)}) async-start(), calls=%async_computation | async-start | bytes 41943040 | tf_op jit(solution)/shard_map/all_gather | solution.py:327
  32.2 22.7 %copy-start.13 = (bf16[4096,8]{0,1:T(8,128)(2,1)S(1)}, bf16[4096,8]{0,1:T(8,128)(2,1)}, u32[]{:S(2)}) copy-start(bf16[4096,8]{0,1:T(8,128)(2,1)} %param.12) | copy-start | bytes 196612
  32.2 668.6 %all-gather.7.cloned.1.call-start = ((), (), s32[]{:S(2)}) async-start(), calls=%async_computation.1 | async-start | bytes 41943040 | tf_op jit(solution)/shard_map/all_gather | solution.py:327
  32.2 59.3 %collective-permute-start.4 = (bf16[2048,4096]{1,0:T(8,128)(2,1)}, bf16[2048,4096]{1,0:T(8,128)(2,1)}, u32[]{:S(2)}, u32[]{:S(2)}) collective-permute-start(bf16[2048,4096]{1,0:T(8,128)(2,1)} %x_ref.1), channel_id=1, source_target_pairs={{0,1},{1,0},{2,3},{3,2},{4,5},{5,4},{6,7},{7,6}} | collective-permute-start | bytes 50331656 | tf_op jit(solution)/shard_map/ppermute | solution.py:328
  40.6 25.1 %copy-start.26 = (pred[16]{0:T(512)(128)(4,1)}, pred[16]{0:T(512)(128)(4,1)S(1)}, u32[]{:S(2)}) copy-start(pred[16]{0:T(512)(128)(4,1)S(1)} %iota_compare_fusion.42) | copy-start | bytes 52
  43.9 21.9 %copy-start.27 = (pred[8]{0:T(512)(128)(4,1)}, pred[8]{0:T(512)(128)(4,1)S(1)}, u32[]{:S(2)}) copy-start(pred[8]{0:T(512)(128)(4,1)S(1)} %iota_compare_fusion.43) | copy-start | bytes 28
  50.1 15.6 %copy-start.19 = (s32[8]{0:T(128)}, s32[8]{0:T(128)S(1)}, u32[]{:S(2)}) copy-start(s32[8]{0:T(128)S(1)} %select_add_fusion) | copy-start | bytes 100
  54.5 10.7 copy-start.18
  54.9 10.9 copy-start.15
  54.9 10.2 copy-start.4
  65.1 23.3 %copy-start.3 = (f32[2048,2]{0,1:T(2,128)}, f32[2048,2]{0,1:T(2,128)S(1)}, u32[]{:S(2)}) copy-start(f32[2048,2]{0,1:T(2,128)S(1)} %select_reduce_fusion.9) | copy-start | bytes 49156
  65.8 6.7 copy-start.20
  70.8 20.8 %copy-start.12 = (s32[8,16]{0,1:T(8,128)}, s32[8,16]{0,1:T(8,128)S(1)}, u32[]{:S(2)}) copy-start(s32[8,16]{0,1:T(8,128)S(1)} %copy.65) | copy-start | bytes 1540
  75.7 15.9 %copy-start.10 = (f32[2048]{0:T(1024)}, f32[2048]{0:T(1024)S(1)}, u32[]{:S(2)}) copy-start(f32[2048]{0:T(1024)S(1)} %reduce_max.55) | copy-start | bytes 24580
  75.9 7.0 copy-start.25
  80.5 3.9 copy-start
  84.4 0.6 copy-start.7
  693.6 3.3 copy-start.6
  693.6 6.3 copy-start.22
  693.6 6.5 copy-start.24
  699.7 265.1 %collective-permute-start.6 = (bf16[832,4096]{1,0:T(8,128)(2,1)}, bf16[832,4096]{1,0:T(8,128)(2,1)}, u32[]{:S(2)}, u32[]{:S(2)}) collective-permute-start(bf16[832,4096]{1,0:T(8,128)(2,1)} %pad_maximum_fusion.5), channel_id=1, source_target_pairs={{0,3},{1,2},{2,1},{3,0},{4,7},{5,6},{6,5},{7,4}} | collective-permute-start | bytes 20447240 | tf_op jit(solution)/shard_map/ppermute | solution.py:412
  699.7 270.0 %collective-permute-start.5 = (bf16[832,4096]{1,0:T(8,128)(2,1)}, bf16[832,4096]{1,0:T(8,128)(2,1)}, u32[]{:S(2)}, u32[]{:S(2)}) collective-permute-start(bf16[832,4096]{1,0:T(8,128)(2,1)} %pad_maximum_fusion.4), channel_id=1, source_target_pairs={{0,2},{1,3},{2,0},{3,1},{4,6},{5,7},{6,4},{7,5}} | collective-permute-start | bytes 20447240 | tf_op jit(solution)/shard_map/ppermute | solution.py:412
  957.3 326.5 %collective-permute-start.9 = (bf16[832,4096]{1,0:T(8,128)(2,1)}, bf16[832,4096]{1,0:T(8,128)(2,1)}, u32[]{:S(2)}, u32[]{:S(2)}) collective-permute-start(bf16[832,4096]{1,0:T(8,128)(2,1)} %pad_maximum_fusion.7), channel_id=1, source_target_pairs={{0,3},{1,2},{2,1},{3,0},{4,7},{5,6},{6,5},{7,4}} | collective-permute-start | bytes 20447240 | tf_op jit(solution)/shard_map/ppermute | solution.py:412
  957.3 12.4 copy-start.9
  957.3 14.6 %copy-start.21 = (s32[8]{0:T(128)S(1)}, s32[8]{0:T(128)}, u32[]{:S(2)}) copy-start(s32[8]{0:T(128)} %get-tuple-element.969) | copy-start | bytes 100
  957.3 15.7 %copy-start.23 = (s32[8]{0:T(128)S(1)}, s32[8]{0:T(128)}, u32[]{:S(2)}) copy-start(s32[8]{0:T(128)} %select_reduce_fusion.31.blk) | copy-start | bytes 100
  960.7 323.1 %collective-permute-start.8 = (bf16[832,4096]{1,0:T(8,128)(2,1)}, bf16[832,4096]{1,0:T(8,128)(2,1)}, u32[]{:S(2)}, u32[]{:S(2)}) collective-permute-start(bf16[832,4096]{1,0:T(8,128)(2,1)} %pad_maximum_fusion.6), channel_id=1, source_target_pairs={{0,2},{1,3},{2,0},{3,1},{4,6},{5,7},{6,4},{7,5}} | collective-permute-start | bytes 20447240 | tf_op jit(solution)/shard_map/ppermute | solution.py:412
  972.1 311.7 %collective-permute-start.7 = (bf16[2048,4096]{1,0:T(8,128)(2,1)}, bf16[2048,4096]{1,0:T(8,128)(2,1)}, u32[]{:S(2)}, u32[]{:S(2)}) collective-permute-start(bf16[2048,4096]{1,0:T(8,128)(2,1)} %ffn.4), channel_id=1, source_target_pairs={{0,1},{1,0},{2,3},{3,2},{4,5},{5,4},{6,7},{7,6}} | collective-permute-start | bytes 50331656 | tf_op jit(solution)/shard_map/ppermute | solution.py:414
Sparse Core Ops, SparseCore 0:
  32.3 199.3 all-gather.4
  233.3 199.3 all-gather.6
